TPU v7x, 8 devices: a whole 2x2x1 slice. The times are simulated.
8 devices in a mesh: dp: 1 (over z), tp: 8 (over y, x, core).
Axes of the slice: x: 2, y: 2, z: 1, core: 2. Of those that a mesh axis runs over, the one named last changes fastest.
Arguments:
- enc_out: bfloat16 [12, 2048, 1024], P('dp', 'tp')
- norm_scale: bfloat16 [1024], replicated
- w_key: bfloat16 [3, 1024, 32, 128], P(None, None, 'tp')
- w_value: bfloat16 [3, 1024, 32, 128], P(None, None, 'tp')
Outputs:
- output 1: bfloat16 [3, 12, 2048, 32, 128], P(None, 'dp', None, 'tp')
- output 2: bfloat16 [3, 12, 2048, 32, 128], P(None, 'dp', None, 'tp')
All inputs are finite; a program needn't handle non-finite values.
Results may differ from a plain program's by a relative error of at most 0.001.
Values are sent between devices in bfloat16 or wider.
A program may use at most 1 GiB of HBM per device.

v0:
```python
import jax
import jax.numpy as jnp
from jax import lax
from jax.sharding import PartitionSpec as P

NORM_EPS = 1e-6


def rms_norm(enc_out, norm_scale):
    acts = enc_out.astype(jnp.float32)
    mean_sq = jnp.mean(acts * acts, axis=-1, keepdims=True)
    return (acts * lax.rsqrt(mean_sq + NORM_EPS) * norm_scale.astype(jnp.float32)).astype(jnp.bfloat16)


def solution(mesh):
    def per_device(enc_out, norm_scale, w_key, w_value):
        normed = rms_norm(enc_out, norm_scale)
        gathered = lax.all_gather(normed, "tp", axis=1, tiled=True)
        key_cache = jnp.einsum("bsd,ldhk->lbshk", gathered, w_key, preferred_element_type=jnp.float32).astype(jnp.bfloat16)
        value_cache = jnp.einsum("bsd,ldhk->lbshk", gathered, w_value, preferred_element_type=jnp.float32).astype(jnp.bfloat16)
        return key_cache, value_cache

    weight_spec = P(None, None, "tp", None)
    cache_spec = P(None, "dp", None, "tp", None)
    return jax.shard_map(per_device, mesh=mesh, in_specs=(P("dp", "tp", None), P(None), weight_spec, weight_spec), out_specs=(cache_spec, cache_spec), check_vma=False)
```

profile of v0, /device:TPU:0, one launch (start us, length us, event | category | flops | bytes accessed | tf_op | source)
XLA Modules:
  0.0 623.7 jit_solution(18330805382788248348)
XLA Ops:
  7.2 0.0 all-gather.2.cloned.1.call-start
  7.2 0.7 convert_element_type.22
  7.9 0.0 copy-start
  7.9 4.2 fusion.8
  12.1 7.2 %fusion.10 = bf16[12,256,1024]{2,1,0:T(8,128)(2,1)} fusion(bf16[12,256,1024]{2,1,0:T(8,128)(2,1)} %param.4, f32[1024]{0:T(1024)S(1)} %convert_element_type.22, f32[12,256]{1,0:T(8,128)S(1)} %add_rsqrt_fusion), kind=kLoop, calls=%fused_computation.10 | loop fusion | flops 12582912 | bytes 12599296 | tf_op jit(solution)/shard_map/convert_element_type | solution.py:12
  19.3 0.0 all-gather.2.cloned.1.call-update
  19.3 229.6 %all-gather.2.cloned.1.call-done = bf16[12,2048,1024]{2,1,0:T(8,128)(2,1)} async-done(((bf16[12,256,1024]{2,1,0:T(8,128)(2,1)}), bf16[12,2048,1024]{2,1,0:T(8,128)(2,1)}) %all-gather.2.cloned.1.call-update) | async-done | bytes 50331664 | tf_op jit(solution)/shard_map/all_gather | solution.py:18
  248.9 0.0 copy-done
  248.9 86.5 %convert_bitcast_fusion = bf16[3,12,2048,4,128]{4,2,3,0,1:T(8,128)(2,1)} fusion(bf16[12,2048,1024]{2,1,0:T(8,128)(2,1)} %all-gather.2.cloned.1.call-done, bf16[3,1024,4,128]{3,2,1,0:T(4,128)(2,1)S(1)} %copy-done), kind=kOutput, calls=%fused_computation | convolution fusion | flops 77347160064 | bytes 128974848 | tf_op jit(solution)/shard_map/bsd,ldhk->lbshk/dot_general | solution.py:20
  335.5 0.0 copy-start.1
  335.5 97.5 %copy.9 = bf16[3,12,2048,4,128]{4,3,2,1,0:T(4,128)(2,1)} copy(bf16[3,12,2048,4,128]{4,2,3,0,1:T(8,128)(2,1)} %convert_bitcast_fusion) | data formatting | bytes 150994944
  433.0 0.0 copy-done.1
  433.0 86.5 %convert_bitcast_fusion.1 = bf16[3,12,2048,4,128]{4,2,3,0,1:T(8,128)(2,1)} fusion(bf16[12,2048,1024]{2,1,0:T(8,128)(2,1)} %all-gather.2.cloned.1.call-done, bf16[3,1024,4,128]{3,2,1,0:T(4,128)(2,1)S(1)} %copy-done.1), kind=kOutput, calls=%fused_computation.1 | convolution fusion | flops 77347160064 | bytes 128974848 | tf_op jit(solution)/shard_map/bsd,ldhk->lbshk/dot_general | solution.py:19
  519.5 97.4 %copy.8 = bf16[3,12,2048,4,128]{4,3,2,1,0:T(4,128)(2,1)} copy(bf16[3,12,2048,4,128]{4,2,3,0,1:T(8,128)(2,1)} %convert_bitcast_fusion.1) | data formatting | bytes 150994944
  (1 shorter events, 0.0 us)
Async XLA Ops:
  7.2 241.8 %all-gather.2.cloned.1.call-start = ((), (), s32[]{:S(2)}) async-start(), calls=%async_computation | async-start | bytes 56623104 | tf_op jit(solution)/shard_map/all_gather | solution.py:18
  7.9 241.0 %copy-start = (bf16[3,1024,4,128]{3,2,1,0:T(4,128)(2,1)S(1)}, bf16[3,1024,4,128]{3,2,1,0:T(4,128)(2,1)}, u32[]{:S(2)}) copy-start(bf16[3,1024,4,128]{3,2,1,0:T(4,128)(2,1)} %param.7) | copy-start | bytes 9437188
  335.5 97.5 %copy-start.1 = (bf16[3,1024,4,128]{3,2,1,0:T(4,128)(2,1)S(1)}, bf16[3,1024,4,128]{3,2,1,0:T(4,128)(2,1)}, u32[]{:S(2)}) copy-start(bf16[3,1024,4,128]{3,2,1,0:T(4,128)(2,1)} %param.6) | copy-start | bytes 9437188
Sparse Core Ops, SparseCore 0:
  19.4 229.4 all-gather.1
where the time goes:
time: 624 us
  waiting for transfers between devices  230 us (37%)
  local copies, waits for them, and re-layouts  195 us (31%)
  matrix products  173 us (28%)
  between operations  14 us (2%)
  other arithmetic  12.1 us (2%)
    all_gather x1, waiting for transfers between devices, per_device(): gathered = lax.all_gather(normed, 'tp', axis=1, tiled=True)  230 us
    unnamed x6, local copies, waits for them, and re-layouts  195 us
    dot_general x1, matrix products, per_device(): jnp.einsum('bsd,ldhk->lbshk', gathered, w_value, preferred_element_type=j...  86.5 us
    dot_general x1, matrix products, per_device(): jnp.einsum('bsd,ldhk->lbshk', gathered, w_key, preferred_element_type=jnp...  86.5 us
  transfers between devices with their start and end apart: 1, of which 1 were waited for; matrix products, arithmetic and copies ran while one was open for 0% of the time, Pallas kernels for 0%

commit v1 on v0

v1 whole, which is shorter than its diff:
```python
import functools

import jax
import jax.numpy as jnp
from jax import lax
from jax.experimental import pallas as pl
from jax.experimental.pallas import tpu as pltpu
from jax.sharding import PartitionSpec as P


NORM_EPS = 1e-6

CORE, NEAR_X, NEAR_Y, DIAGONAL = 1, 2, 4, 6
BATCHES_PER_UNIT = 2
PIECES = (4, 2)
ORDER = ("a0", "b0", "a1", "f0", "b1", "f1")

HBM = pl.BlockSpec(memory_space=pltpu.HBM)
VMEM = pl.BlockSpec(memory_space=pltpu.VMEM)


def rms_norm(enc_out, norm_scale):
    acts = enc_out.astype(jnp.float32)
    mean_sq = jnp.mean(acts * acts, axis=-1, keepdims=True)
    return (acts * lax.rsqrt(mean_sq + NORM_EPS) * norm_scale.astype(jnp.float32)).astype(jnp.bfloat16)


def norm_kernel(*refs):
    n = len(refs) // 2
    for x_ref, y_ref in zip(refs[:n], refs[n + 1 :]):
        y_ref[...] = rms_norm(x_ref[...], refs[n][...])


def normalize(enc_out, norm_scale, first, n):
    _, seq, width = enc_out.shape
    return pl.pallas_call(
        norm_kernel,
        out_shape=[jax.ShapeDtypeStruct((n, seq, width), jnp.bfloat16) for _ in first],
        grid=(n,),
        in_specs=[pl.BlockSpec((1, seq, width), functools.partial(lambda f, i: (f + i, 0, 0), f)) for f in first]
        + [pl.BlockSpec((1, width), lambda i: (0, 0))],
        out_specs=[pl.BlockSpec((1, seq, width), lambda i: (i, 0, 0)) for _ in first],
        cost_estimate=pl.CostEstimate(flops=8 * len(first) * n * seq * width, bytes_accessed=4 * len(first) * n * seq * width, transcendentals=0),
        name="normalize",
    )(*[enc_out] * len(first), norm_scale.reshape(1, width))


def together(*values):
    return lax.optimization_barrier(values)


def pick(n, values):
    out = values[-1]
    for k in range(len(values) - 2, -1, -1):
        out = jnp.where(n == k, values[k], out)
    return out


def project_kernel(plan, n_layers, *refs):
    n_arrays, group = len(plan), BATCHES_PER_UNIT
    arrays, weights = refs[:n_arrays], refs[n_arrays : n_arrays + 2]
    *outs, tokens, rounded, in_sem, out_sem = refs[-6:]
    seq = arrays[0].shape[1]
    rows = rounded.shape[2] // group
    me = lax.axis_index("tp")
    flat = [(a, e, first + e, mask) for a, (n, first, mask) in enumerate(plan) for e in range(n)]
    units = [flat[k : k + group] for k in range(0, len(flat), group)]

    def load(n, slot):
        for k, unit in enumerate(units):

            @pl.when(n == k)
            def _():
                for g, (a, e, _, _) in enumerate(unit):
                    pltpu.make_async_copy(arrays[a].at[e], tokens.at[slot, pl.ds(g * seq, seq)], in_sem.at[slot, g]).start()

    def stores(n, slot):
        for g in range(group):
            entry = pick(n, [unit[g][2] for unit in units])
            source = me ^ pick(n, [unit[g][3] for unit in units])
            for j in range(2 * n_layers):
                to = outs[j % 2].at[j // 2, entry, pl.ds(pl.multiple_of(source * rows, rows), rows)]
                yield pltpu.make_async_copy(rounded.at[slot, j, pl.ds(g * rows, rows)], to, out_sem.at[slot, j, g])

    load(0, 0)

    def body(n, _):
        slot = lax.rem(n, 2)
        for g in range(group):
            pltpu.make_async_copy(arrays[0].at[0], tokens.at[slot, pl.ds(g * seq, seq)], in_sem.at[slot, g]).wait()

        @pl.when(n + 1 < len(units))
        def _():
            load(n + 1, 1 - slot)

        @pl.when(n >= 2)
        def _():
            for copy in stores(n, slot):
                copy.wait()

        x = tokens[slot]
        for j in range(2 * n_layers):
            product = jnp.dot(x, weights[j % 2][j // 2], preferred_element_type=jnp.float32)
            rounded[slot, j] = product.reshape(rounded.shape[2:]).astype(jnp.bfloat16)
        for copy in stores(n, slot):
            copy.start()
        return 0

    lax.fori_loop(0, len(units), body, 0)
    for n in range(max(len(units) - 2, 0), len(units)):
        for copy in stores(n, n % 2):
            copy.wait()


def project(arrays, plan, weights, caches, cache_shape):
    n_arrays, group = len(arrays), BATCHES_PER_UNIT
    n_layers, width, columns = weights[0].shape
    seq = arrays[0].shape[1]
    rows, lanes = group * seq * columns // 128, 128
    entries = sum(n for n, _, _ in plan)
    arrays = [pltpu.with_memory_space_constraint(a, pltpu.HBM) for a in arrays]
    weights = [pltpu.with_memory_space_constraint(w, pltpu.VMEM) for w in weights]
    return pl.pallas_call(
        functools.partial(project_kernel, plan, n_layers),
        out_shape=[jax.ShapeDtypeStruct(cache_shape, jnp.bfloat16)] * 2,
        in_specs=[HBM] * n_arrays + [VMEM, VMEM] + [HBM] * len(caches),
        out_specs=[HBM, HBM],
        input_output_aliases={n_arrays + 2 + i: i for i in range(len(caches))},
        scratch_shapes=[
            pltpu.VMEM((2, group * seq, width), jnp.bfloat16),
            pltpu.VMEM((2, 2 * n_layers, rows, lanes), jnp.bfloat16),
            pltpu.SemaphoreType.DMA((2, group)),
            pltpu.SemaphoreType.DMA((2, 2 * n_layers, group)),
        ],
        compiler_params=pltpu.CompilerParams(vmem_limit_bytes=57 * 2**20),
        cost_estimate=pl.CostEstimate(
            flops=2 * entries * seq * width * columns * 2 * n_layers,
            bytes_accessed=2 * entries * seq * (width + columns * 2 * n_layers),
            transcendentals=0,
        ),
    )(*arrays, *weights, *caches)


def solution(mesh):
    def per_device(enc_out, norm_scale, w_key, w_value):
        n_batch, seq, width = enc_out.shape
        n_layers, _, heads, head_dim = w_key.shape
        n_dev = mesh.shape["tp"]

        def swap(a, mask):
            return lax.ppermute(a, "tp", [(i, i ^ mask) for i in range(n_dev)])

        first = [sum(PIECES[:k]) for k in range(len(PIECES))]
        half = sum(PIECES)
        own, spans = ([], []), ([], [])
        for f, n in zip(first, PIECES):
            for s, y in enumerate(normalize(enc_out, norm_scale, (f, half + f), n)):
                own[s].append(y)
                spans[s].append((n, s * half + f))

        arrived = {}

        def send(what):
            for link, mask in ((0, NEAR_X), (1, NEAR_Y)):
                kind, k = what[0], int(what[1])
                if kind == "f":
                    array, span, _ = arrived[1 - link, f"a{k}"]
                    arrived[link, what] = [swap(array, mask), span, DIAGONAL]
                else:
                    s = link if kind == "a" else 1 - link
                    arrived[link, what] = [swap(own[s][k], mask), spans[s][k], mask]

        def to_partner(group):
            return [[swap(a, CORE), span, mask ^ CORE] for a, span, mask in group]

        for what in ORDER:
            if what[0] != "f":
                send(what)
        mine = [[own[s][k], spans[s][k], 0] for s in (0, 1) for k in range(len(PIECES))]
        theirs = to_partner(mine)
        *_, w_key, w_value = together(*[y for ys in own for y in ys], w_key, w_value)
        weights = [w.reshape(n_layers, width, heads * head_dim) for w in (w_key, w_value)]
        cache_shape, caches = (n_layers, n_batch, n_dev * seq * heads, head_dim), ()

        def call(group, caches):
            return project([a for a, _, _ in group], [(*span, mask) for _, span, mask in group], weights, caches, cache_shape)

        caches = call(mine, caches)
        caches = call(theirs, caches)
        waiting = []
        for what in ORDER:
            group = [arrived[link, what] for link in (0, 1)]
            group[0][0], group[1][0], *caches = together(group[0][0], group[1][0], *caches)
            if what[0] == "a":
                send("f" + what[1])
            to_come = to_partner(group)
            caches = call(waiting + group, caches)
            waiting = to_come
        caches = call(waiting, caches)
        return tuple(c.reshape(n_layers, n_batch, n_dev * seq, heads, head_dim) for c in caches)

    weight_spec = P(None, None, "tp", None)
    cache_spec = P(None, "dp", None, "tp", None)
    return jax.shard_map(per_device, mesh=mesh, in_specs=(P("dp", "tp", None), P(None), weight_spec, weight_spec), out_specs=(cache_spec, cache_spec), check_vma=False)
```

time: 624 us -> 270 us (0.43)
  Pallas kernels: 0 us -> 206 us
  waiting for transfers between devices: 230 us -> 32.2 us
  local copies, waits for them, and re-layouts: 195 us -> 10.4 us
  matrix products: 173 us -> 0 us
  starting transfers between devices: 0.04 us -> 19.9 us
  between operations: 14 us -> 1.01 us
  other arithmetic: 12.1 us -> 0 us
    all_gather x1 -> x0, waiting for transfers between devices: 230 us -> none  [per_device(): gathered = lax.all_gather(normed, 'tp', axis=1, tiled=True)]
    pallas_call x0 -> x11, Pallas kernels: none -> 206 us  [the longest x9 197 us: project(): pl.pallas_call(functools.partial(project_kernel, plan, n_layers), out_sha...]
    unnamed x6 -> x4, local copies, waits for them, and re-layouts: 195 us -> 1.89 us
    dot_general x2 -> x0, matrix products: 173 us -> none  [the longest x1 86.5 us: per_device(): jnp.einsum('bsd,ldhk->lbshk', gathered, w_value, preferred_element_type=j...]
    ppermute x0 -> x28, waiting for transfers between devices: none -> 32.2 us  [swap(): return lax.ppermute(a, 'tp', [(i, i ^ mask) for i in range(n_dev)])]
    ppermute x0 -> x28, starting transfers between devices: none -> 19.9 us  [swap(): return lax.ppermute(a, 'tp', [(i, i ^ mask) for i in range(n_dev)])]
    reshape x0 -> x3, local copies, waits for them, and re-layouts: none -> 8.48 us  [the longest x2 7.2 us: per_device(): w.reshape(n_layers, width, heads * head_dim)]
    convert_element_type x2 -> x0, other arithmetic: 7.84 us -> none  [the longest x1 7.15 us: rms_norm(): (acts * lax.rsqrt(mean_sq + NORM_EPS) * norm_scale.astype(jnp.float32)).a...]
  transfers between devices with their start and end apart: 1 -> 28, of which waited for: 1 -> 3; matrix products, arithmetic and copies ran while one was open for 0% -> 3% of each run, Pallas kernels for 0% -> 72%
where the time goes in v1:
time: 270 us; the launch traced here: 269 us
  Pallas kernels  206 us (76%)
  waiting for transfers between devices  32.2 us (12%)
  starting transfers between devices  19.9 us (7%)
  local copies, waits for them, and re-layouts  10.4 us (4%)
    pallas_call x9, Pallas kernels, project(): pl.pallas_call(functools.partial(project_kernel, plan, n_layers), out_sha...  197 us
    ppermute x28, waiting for transfers between devices, swap(): return lax.ppermute(a, 'tp', [(i, i ^ mask) for i in range(n_dev)])  32.2 us
    ppermute x28, starting transfers between devices, swap(): return lax.ppermute(a, 'tp', [(i, i ^ mask) for i in range(n_dev)])  19.9 us
    pallas_call x2, Pallas kernels, normalize(): pl.pallas_call(norm_kernel, out_shape=[jax.ShapeDtypeStruct((n, seq, widt...  8.36 us
    reshape x2, local copies, waits for them, and re-layouts, per_device(): w.reshape(n_layers, width, heads * head_dim)  7.2 us
  transfers between devices with their start and end apart: 28, of which 3 were waited for; matrix products, arithmetic and copies ran while one was open for 3% of the time, Pallas kernels for 72%

profile of v1, /device:TPU:0, one launch (start us, length us, event | category | flops | bytes accessed | tf_op | source)
XLA Modules:
  0.0 269.0 jit_solution(16839161161767973653)
XLA Ops:
  0.6 1.3 reshape.20.refs_2_
  1.9 3.0 %normalize.2 = (bf16[2,256,1024]{2,1,0:T(8,128)(2,1)}, bf16[2,256,1024]{2,1,0:T(8,128)(2,1)}) custom-call(bf16[12,256,1024]{2,1,0:T(8,128)(2,1)} %refs_1_.3, bf16[12,256,1024]{2,1,0:T(8,128)(2,1)} %refs_1_.3, bf16[1,1024]{1,0:T(2,128)(2,1)} %reshape.20.refs_2_), custom_call_target="tpu_custom_call" | custom-call | flops 8388608 | bytes 4194304 | tf_op jit(solution)/shard_map/normalize/pallas_call | solution.py:36
  4.9 0.8 collective-permute-start.5
  5.7 5.4 %normalize.3 = (bf16[4,256,1024]{2,1,0:T(8,128)(2,1)}, bf16[4,256,1024]{2,1,0:T(8,128)(2,1)}) custom-call(bf16[12,256,1024]{2,1,0:T(8,128)(2,1)} %refs_1_.3, bf16[12,256,1024]{2,1,0:T(8,128)(2,1)} %refs_1_.3, bf16[1,1024]{1,0:T(2,128)(2,1)} %reshape.20.refs_2_), custom_call_target="tpu_custom_call" | custom-call | flops 16777216 | bytes 8388608 | tf_op jit(solution)/shard_map/normalize/pallas_call | solution.py:36
  11.1 0.1 collective-permute-start.4
  11.2 0.4 collective-permute-start.6
  11.6 2.6 collective-permute-start.2
  14.3 0.2 collective-permute-start.7
  14.5 3.2 %reshape.21.refs_4_.refs_2_ = bf16[3,1024,512]{2,1,0:T(8,128)(2,1)} reshape(bf16[3,1024,4,128]{3,2,1,0:T(4,128)(2,1)S(1)} %copy-done.1) | data formatting | bytes 6291456 | tf_op jit(solution)/shard_map/reshape | solution.py:182
  17.7 4.0 %reshape.22.refs_5_.refs_3_ = bf16[3,1024,512]{2,1,0:T(8,128)(2,1)S(1)} reshape(bf16[3,1024,4,128]{3,2,1,0:T(4,128)(2,1)} %param.7) | data formatting | bytes 6291456 | tf_op jit(solution)/shard_map/reshape | solution.py:182
  21.7 0.0 collective-permute-done.5.refs_1_
  21.7 1.5 collective-permute-start.3
  23.2 1.9 copy-done
  25.1 24.3 %shard_map.59 = (bf16[3,12,8192,128]{3,2,1,0:T(8,128)(2,1)}, bf16[3,12,8192,128]{3,2,1,0:T(8,128)(2,1)}) custom-call(bf16[4,256,1024]{2,1,0:T(8,128)(2,1)} %get-tuple-element.52.refs_0_, bf16[2,256,1024]{2,1,0:T(8,128)(2,1)} %get-tuple-element.50.refs_1_, bf16[4,256,1024]{2,1,0:T(8,128)(2,1)} %get-tuple-element.53.refs_2_, ...), custom_call_target="tpu_custom_call" | custom-call | flops 19327352832 | bytes 25165824 | tf_op jit(solution)/shard_map/pallas_call | solution.py:123
  49.4 0.0 collective-permute-done.7.refs_3_
  49.4 0.6 collective-permute-start.10
  50.0 0.0 collective-permute-done.4.refs_0_
  50.0 0.3 collective-permute-start.11
  50.2 0.0 collective-permute-done.6.refs_2_
  50.2 24.3 %shard_map.60 = (bf16[3,12,8192,128]{3,2,1,0:T(8,128)(2,1)}, bf16[3,12,8192,128]{3,2,1,0:T(8,128)(2,1)}) custom-call(bf16[4,256,1024]{2,1,0:T(8,128)(2,1)} %collective-permute-done.4.refs_0_, bf16[2,256,1024]{2,1,0:T(8,128)(2,1)} %collective-permute-done.5.refs_1_, ...), custom_call_target="tpu_custom_call", output_to_operand_aliasing={{0}: (6, {}), {1}: (7, {})} | custom-call | flops 19327352832 | bytes 25165824 | tf_op jit(solution)/shard_map/pallas_call | solution.py:123
  74.5 0.0 collective-permute-done.2.refs_0_
  74.5 0.0 collective-permute-done.3.refs_1_
  74.5 0.0 collective-permute-start.8
  74.6 0.5 collective-permute-start.9
  75.1 1.7 collective-permute-start
  76.8 17.2 %shard_map.61 = (bf16[3,12,8192,128]{3,2,1,0:T(8,128)(2,1)}, bf16[3,12,8192,128]{3,2,1,0:T(8,128)(2,1)}) custom-call(bf16[4,256,1024]{2,1,0:T(8,128)(2,1)} %collective-permute-done.2.refs_0_, bf16[4,256,1024]{2,1,0:T(8,128)(2,1)} %collective-permute-done.3.refs_1_, bf16[3,1024,512]{2,1,0:T(8,128)(2,1)S(1)} %copy-done, ...), custom_call_target="tpu_custom_call", output_to_operand_aliasing={{0}: (4, {}), {1}: (5, {})} | custom-call | flops 12884901888 | bytes 16777216 | tf_op jit(solution)/shard_map/pallas_call | solution.py:123
  94.0 12.0 %collective-permute-done.10.refs_2_ = bf16[4,256,1024]{2,1,0:T(8,128)(2,1)} collective-permute-done((bf16[4,256,1024]{2,1,0:T(8,128)(2,1)}, bf16[4,256,1024]{2,1,0:T(8,128)(2,1)}, u32[]{:S(2)}, u32[]{:S(2)}) %collective-permute-start.10) | collective-permute-done | bytes 2097184 | tf_op jit(solution)/shard_map/ppermute | solution.py:151
  106.0 2.1 collective-permute-start.1
  108.0 7.4 %collective-permute-done.11.refs_3_ = bf16[4,256,1024]{2,1,0:T(8,128)(2,1)} collective-permute-done((bf16[4,256,1024]{2,1,0:T(8,128)(2,1)}, bf16[4,256,1024]{2,1,0:T(8,128)(2,1)}, u32[]{:S(2)}, u32[]{:S(2)}) %collective-permute-start.11) | collective-permute-done | bytes 2097184 | tf_op jit(solution)/shard_map/ppermute | solution.py:151
  115.5 0.3 collective-permute-start.14
  115.8 12.7 %collective-permute-done.refs_2_ = bf16[2,256,1024]{2,1,0:T(8,128)(2,1)} collective-permute-done((bf16[2,256,1024]{2,1,0:T(8,128)(2,1)}, bf16[2,256,1024]{2,1,0:T(8,128)(2,1)}, u32[]{:S(2)}, u32[]{:S(2)}) %collective-permute-start) | collective-permute-done | bytes 1048608 | tf_op jit(solution)/shard_map/ppermute | solution.py:151
  128.5 2.1 collective-permute-start.15
  130.5 0.0 collective-permute-done.8.refs_0_
  130.5 0.0 collective-permute-start.16
  130.5 0.0 collective-permute-done.9.refs_1_
  130.5 0.5 collective-permute-start.17
  131.0 31.4 %shard_map.62 = (bf16[3,12,8192,128]{3,2,1,0:T(8,128)(2,1)}, bf16[3,12,8192,128]{3,2,1,0:T(8,128)(2,1)}) custom-call(bf16[4,256,1024]{2,1,0:T(8,128)(2,1)} %collective-permute-done.8.refs_0_, bf16[4,256,1024]{2,1,0:T(8,128)(2,1)} %collective-permute-done.9.refs_1_, ...), custom_call_target="tpu_custom_call", output_to_operand_aliasing={{0}: (6, {}), {1}: (7, {})} | custom-call | flops 25769803776 | bytes 33554432 | tf_op jit(solution)/shard_map/pallas_call | solution.py:123
  162.4 0.0 collective-permute-done.1.refs_3_
  162.4 0.0 collective-permute-start.22
  162.5 0.0 collective-permute-done.16.refs_0_
  162.5 0.5 collective-permute-start.23
  163.0 0.0 collective-permute-done.17.refs_1_
  163.0 24.3 %shard_map.63 = (bf16[3,12,8192,128]{3,2,1,0:T(8,128)(2,1)}, bf16[3,12,8192,128]{3,2,1,0:T(8,128)(2,1)}) custom-call(bf16[4,256,1024]{2,1,0:T(8,128)(2,1)} %collective-permute-done.16.refs_0_, bf16[4,256,1024]{2,1,0:T(8,128)(2,1)} %collective-permute-done.17.refs_1_, ...), custom_call_target="tpu_custom_call", output_to_operand_aliasing={{0}: (6, {}), {1}: (7, {})} | custom-call | flops 19327352832 | bytes 25165824 | tf_op jit(solution)/shard_map/pallas_call | solution.py:123
  187.2 0.0 collective-permute-done.14.refs_2_
  187.2 0.0 collective-permute-done.15.refs_3_
  187.3 0.1 collective-permute-start.18
  187.3 0.5 collective-permute-start.19
  187.8 1.5 collective-permute-start.20
  189.3 0.0 collective-permute-done.22.refs_0_
  189.3 0.5 collective-permute-start.21
  189.8 0.0 collective-permute-done.23.refs_1_
  189.8 0.1 collective-permute-start.12
  189.9 24.3 %shard_map.64 = (bf16[3,12,8192,128]{3,2,1,0:T(8,128)(2,1)}, bf16[3,12,8192,128]{3,2,1,0:T(8,128)(2,1)}) custom-call(bf16[2,256,1024]{2,1,0:T(8,128)(2,1)} %collective-permute-done.22.refs_0_, bf16[2,256,1024]{2,1,0:T(8,128)(2,1)} %collective-permute-done.23.refs_1_, ...), custom_call_target="tpu_custom_call", output_to_operand_aliasing={{0}: (6, {}), {1}: (7, {})} | custom-call | flops 19327352832 | bytes 25165824 | tf_op jit(solution)/shard_map/pallas_call | solution.py:123
  214.1 0.0 collective-permute-done.20.refs_2_
  214.1 2.0 collective-permute-start.13
  216.2 0.5 collective-permute-start.27
  216.7 24.3 %shard_map.65 = (bf16[3,12,8192,128]{3,2,1,0:T(8,128)(2,1)}, bf16[3,12,8192,128]{3,2,1,0:T(8,128)(2,1)}) custom-call(bf16[4,256,1024]{2,1,0:T(8,128)(2,1)} %collective-permute-done.18.refs_0_, bf16[4,256,1024]{2,1,0:T(8,128)(2,1)} %collective-permute-done.19.refs_1_, ...), custom_call_target="tpu_custom_call", output_to_operand_aliasing={{0}: (6, {}), {1}: (7, {})} | custom-call | flops 19327352832 | bytes 25165824 | tf_op jit(solution)/shard_map/pallas_call | solution.py:123
  240.9 0.0 collective-permute-done.12.refs_2_
  241.0 0.0 collective-permute-start.24
  241.0 0.5 collective-permute-start.25
  241.5 0.0 collective-permute-done.26.refs_0_
  241.5 0.0 collective-permute-done.27.refs_1_
  241.5 17.2 %shard_map.66 = (bf16[3,12,8192,128]{3,2,1,0:T(8,128)(2,1)}, bf16[3,12,8192,128]{3,2,1,0:T(8,128)(2,1)}) custom-call(bf16[2,256,1024]{2,1,0:T(8,128)(2,1)} %collective-permute-done.26.refs_0_, bf16[2,256,1024]{2,1,0:T(8,128)(2,1)} %collective-permute-done.27.refs_1_, ...), custom_call_target="tpu_custom_call", output_to_operand_aliasing={{0}: (6, {}), {1}: (7, {})} | custom-call | flops 12884901888 | bytes 16777216 | tf_op jit(solution)/shard_map/pallas_call | solution.py:123
  258.7 10.1 %shard_map.67 = (bf16[3,12,8192,128]{3,2,1,0:T(8,128)(2,1)}, bf16[3,12,8192,128]{3,2,1,0:T(8,128)(2,1)}) custom-call(bf16[2,256,1024]{2,1,0:T(8,128)(2,1)} %collective-permute-done.24.refs_0_, bf16[2,256,1024]{2,1,0:T(8,128)(2,1)} %collective-permute-done.25.refs_1_, ...), custom_call_target="tpu_custom_call", output_to_operand_aliasing={{0}: (4, {}), {1}: (5, {})} | custom-call | flops 6442450944 | bytes 8388608 | tf_op jit(solution)/shard_map/pallas_call | solution.py:123
  (10 shorter events, 0.0 us)
Async XLA Ops:
  4.9 9.6 %copy-start.1 = (bf16[3,1024,4,128]{3,2,1,0:T(4,128)(2,1)S(1)}, bf16[3,1024,4,128]{3,2,1,0:T(4,128)(2,1)}, u32[]{:S(2)}) copy-start(bf16[3,1024,4,128]{3,2,1,0:T(4,128)(2,1)} %param.6) | copy-start | bytes 9437188
  4.9 16.8 %collective-permute-start.5 = (bf16[2,256,1024]{2,1,0:T(8,128)(2,1)}, bf16[2,256,1024]{2,1,0:T(8,128)(2,1)}, u32[]{:S(2)}, u32[]{:S(2)}) collective-permute-start(bf16[2,256,1024]{2,1,0:T(8,128)(2,1)} %get-tuple-element.50.refs_1_), channel_id=1, source_target_pairs={{0,1},{1,0},{2,3},{3,2},{4,5},{5,4},{6,7},{7,6}} | collective-permute-start | bytes 3145736 | tf_op jit(solution)/shard_map/ppermute | solution.py:151
  11.1 38.9 %collective-permute-start.4 = (bf16[4,256,1024]{2,1,0:T(8,128)(2,1)}, bf16[4,256,1024]{2,1,0:T(8,128)(2,1)}, u32[]{:S(2)}, u32[]{:S(2)}) collective-permute-start(bf16[4,256,1024]{2,1,0:T(8,128)(2,1)} %get-tuple-element.52.refs_0_), channel_id=1, source_target_pairs={{0,1},{1,0},{2,3},{3,2},{4,5},{5,4},{6,7},{7,6}} | collective-permute-start | bytes 6291464 | tf_op jit(solution)/shard_map/ppermute | solution.py:151
  11.2 39.1 %collective-permute-start.6 = (bf16[4,256,1024]{2,1,0:T(8,128)(2,1)}, bf16[4,256,1024]{2,1,0:T(8,128)(2,1)}, u32[]{:S(2)}, u32[]{:S(2)}) collective-permute-start(bf16[4,256,1024]{2,1,0:T(8,128)(2,1)} %get-tuple-element.53.refs_2_), channel_id=1, source_target_pairs={{0,1},{1,0},{2,3},{3,2},{4,5},{5,4},{6,7},{7,6}} | collective-permute-start | bytes 6291464 | tf_op jit(solution)/shard_map/ppermute | solution.py:151
  11.6 62.9 %collective-permute-start.2 = (bf16[4,256,1024]{2,1,0:T(8,128)(2,1)}, bf16[4,256,1024]{2,1,0:T(8,128)(2,1)}, u32[]{:S(2)}, u32[]{:S(2)}) collective-permute-start(bf16[4,256,1024]{2,1,0:T(8,128)(2,1)} %get-tuple-element.52.refs_0_), channel_id=1, source_target_pairs={{0,2},{1,3},{2,0},{3,1},{4,6},{5,7},{6,4},{7,5}} | collective-permute-start | bytes 6291464 | tf_op jit(solution)/shard_map/ppermute | solution.py:151
  14.3 35.2 %collective-permute-start.7 = (bf16[2,256,1024]{2,1,0:T(8,128)(2,1)}, bf16[2,256,1024]{2,1,0:T(8,128)(2,1)}, u32[]{:S(2)}, u32[]{:S(2)}) collective-permute-start(bf16[2,256,1024]{2,1,0:T(8,128)(2,1)} %get-tuple-element.51.refs_3_), channel_id=1, source_target_pairs={{0,1},{1,0},{2,3},{3,2},{4,5},{5,4},{6,7},{7,6}} | collective-permute-start | bytes 3145736 | tf_op jit(solution)/shard_map/ppermute | solution.py:151
  21.7 52.8 %collective-permute-start.3 = (bf16[4,256,1024]{2,1,0:T(8,128)(2,1)}, bf16[4,256,1024]{2,1,0:T(8,128)(2,1)}, u32[]{:S(2)}, u32[]{:S(2)}) collective-permute-start(bf16[4,256,1024]{2,1,0:T(8,128)(2,1)} %get-tuple-element.53.refs_2_), channel_id=1, source_target_pairs={{0,4},{1,5},{2,6},{3,7},{4,0},{5,1},{6,2},{7,3}} | collective-permute-start | bytes 6291464 | tf_op jit(solution)/shard_map/ppermute | solution.py:151
  23.2 1.9 copy-start
  49.4 56.6 %collective-permute-start.10 = (bf16[4,256,1024]{2,1,0:T(8,128)(2,1)}, bf16[4,256,1024]{2,1,0:T(8,128)(2,1)}, u32[]{:S(2)}, u32[]{:S(2)}) collective-permute-start(bf16[4,256,1024]{2,1,0:T(8,128)(2,1)} %get-tuple-element.53.refs_2_), channel_id=1, source_target_pairs={{0,2},{1,3},{2,0},{3,1},{4,6},{5,7},{6,4},{7,5}} | collective-permute-start | bytes 6291464 | tf_op jit(solution)/shard_map/ppermute | solution.py:151
  50.0 65.5 %collective-permute-start.11 = (bf16[4,256,1024]{2,1,0:T(8,128)(2,1)}, bf16[4,256,1024]{2,1,0:T(8,128)(2,1)}, u32[]{:S(2)}, u32[]{:S(2)}) collective-permute-start(bf16[4,256,1024]{2,1,0:T(8,128)(2,1)} %get-tuple-element.52.refs_0_), channel_id=1, source_target_pairs={{0,4},{1,5},{2,6},{3,7},{4,0},{5,1},{6,2},{7,3}} | collective-permute-start | bytes 6291464 | tf_op jit(solution)/shard_map/ppermute | solution.py:151
  74.5 56.0 %collective-permute-start.8 = (bf16[4,256,1024]{2,1,0:T(8,128)(2,1)}, bf16[4,256,1024]{2,1,0:T(8,128)(2,1)}, u32[]{:S(2)}, u32[]{:S(2)}) collective-permute-start(bf16[4,256,1024]{2,1,0:T(8,128)(2,1)} %collective-permute-done.2.refs_0_), channel_id=1, source_target_pairs={{0,1},{1,0},{2,3},{3,2},{4,5},{5,4},{6,7},{7,6}} | collective-permute-start | bytes 6291464 | tf_op jit(solution)/shard_map/ppermute | solution.py:151
  74.6 55.9 %collective-permute-start.9 = (bf16[4,256,1024]{2,1,0:T(8,128)(2,1)}, bf16[4,256,1024]{2,1,0:T(8,128)(2,1)}, u32[]{:S(2)}, u32[]{:S(2)}) collective-permute-start(bf16[4,256,1024]{2,1,0:T(8,128)(2,1)} %collective-permute-done.3.refs_1_), channel_id=1, source_target_pairs={{0,1},{1,0},{2,3},{3,2},{4,5},{5,4},{6,7},{7,6}} | collective-permute-start | bytes 6291464 | tf_op jit(solution)/shard_map/ppermute | solution.py:151
  75.1 53.4 %collective-permute-start = (bf16[2,256,1024]{2,1,0:T(8,128)(2,1)}, bf16[2,256,1024]{2,1,0:T(8,128)(2,1)}, u32[]{:S(2)}, u32[]{:S(2)}) collective-permute-start(bf16[2,256,1024]{2,1,0:T(8,128)(2,1)} %get-tuple-element.50.refs_1_), channel_id=1, source_target_pairs={{0,2},{1,3},{2,0},{3,1},{4,6},{5,7},{6,4},{7,5}} | collective-permute-start | bytes 3145736 | tf_op jit(solution)/shard_map/ppermute | solution.py:151
  106.0 56.4 %collective-permute-start.1 = (bf16[2,256,1024]{2,1,0:T(8,128)(2,1)}, bf16[2,256,1024]{2,1,0:T(8,128)(2,1)}, u32[]{:S(2)}, u32[]{:S(2)}) collective-permute-start(bf16[2,256,1024]{2,1,0:T(8,128)(2,1)} %get-tuple-element.51.refs_3_), channel_id=1, source_target_pairs={{0,4},{1,5},{2,6},{3,7},{4,0},{5,1},{6,2},{7,3}} | collective-permute-start | bytes 3145736 | tf_op jit(solution)/shard_map/ppermute | solution.py:151
  115.5 71.8 %collective-permute-start.14 = (bf16[4,256,1024]{2,1,0:T(8,128)(2,1)}, bf16[4,256,1024]{2,1,0:T(8,128)(2,1)}, u32[]{:S(2)}, u32[]{:S(2)}) collective-permute-start(bf16[4,256,1024]{2,1,0:T(8,128)(2,1)} %collective-permute-done.3.refs_1_), channel_id=1, source_target_pairs={{0,2},{1,3},{2,0},{3,1},{4,6},{5,7},{6,4},{7,5}} | collective-permute-start | bytes 6291464 | tf_op jit(solution)/shard_map/ppermute | solution.py:151
  128.5 58.8 %collective-permute-start.15 = (bf16[4,256,1024]{2,1,0:T(8,128)(2,1)}, bf16[4,256,1024]{2,1,0:T(8,128)(2,1)}, u32[]{:S(2)}, u32[]{:S(2)}) collective-permute-start(bf16[4,256,1024]{2,1,0:T(8,128)(2,1)} %collective-permute-done.2.refs_0_), channel_id=1, source_target_pairs={{0,4},{1,5},{2,6},{3,7},{4,0},{5,1},{6,2},{7,3}} | collective-permute-start | bytes 6291464 | tf_op jit(solution)/shard_map/ppermute | solution.py:151
  130.5 32.0 %collective-permute-start.16 = (bf16[4,256,1024]{2,1,0:T(8,128)(2,1)}, bf16[4,256,1024]{2,1,0:T(8,128)(2,1)}, u32[]{:S(2)}, u32[]{:S(2)}) collective-permute-start(bf16[4,256,1024]{2,1,0:T(8,128)(2,1)} %collective-permute-done.10.refs_2_), channel_id=1, source_target_pairs={{0,1},{1,0},{2,3},{3,2},{4,5},{5,4},{6,7},{7,6}} | collective-permute-start | bytes 6291464 | tf_op jit(solution)/shard_map/ppermute | solution.py:151
  130.5 32.4 %collective-permute-start.17 = (bf16[4,256,1024]{2,1,0:T(8,128)(2,1)}, bf16[4,256,1024]{2,1,0:T(8,128)(2,1)}, u32[]{:S(2)}, u32[]{:S(2)}) collective-permute-start(bf16[4,256,1024]{2,1,0:T(8,128)(2,1)} %collective-permute-done.11.refs_3_), channel_id=1, source_target_pairs={{0,1},{1,0},{2,3},{3,2},{4,5},{5,4},{6,7},{7,6}} | collective-permute-start | bytes 6291464 | tf_op jit(solution)/shard_map/ppermute | solution.py:151
  162.4 26.9 %collective-permute-start.22 = (bf16[2,256,1024]{2,1,0:T(8,128)(2,1)}, bf16[2,256,1024]{2,1,0:T(8,128)(2,1)}, u32[]{:S(2)}, u32[]{:S(2)}) collective-permute-start(bf16[2,256,1024]{2,1,0:T(8,128)(2,1)} %collective-permute-done.refs_2_), channel_id=1, source_target_pairs={{0,1},{1,0},{2,3},{3,2},{4,5},{5,4},{6,7},{7,6}} | collective-permute-start | bytes 3145736 | tf_op jit(solution)/shard_map/ppermute | solution.py:151
  162.5 27.3 %collective-permute-start.23 = (bf16[2,256,1024]{2,1,0:T(8,128)(2,1)}, bf16[2,256,1024]{2,1,0:T(8,128)(2,1)}, u32[]{:S(2)}, u32[]{:S(2)}) collective-permute-start(bf16[2,256,1024]{2,1,0:T(8,128)(2,1)} %collective-permute-done.1.refs_3_), channel_id=1, source_target_pairs={{0,1},{1,0},{2,3},{3,2},{4,5},{5,4},{6,7},{7,6}} | collective-permute-start | bytes 3145736 | tf_op jit(solution)/shard_map/ppermute | solution.py:151
  187.3 28.9 %collective-permute-start.18 = (bf16[4,256,1024]{2,1,0:T(8,128)(2,1)}, bf16[4,256,1024]{2,1,0:T(8,128)(2,1)}, u32[]{:S(2)}, u32[]{:S(2)}) collective-permute-start(bf16[4,256,1024]{2,1,0:T(8,128)(2,1)} %collective-permute-done.14.refs_2_), channel_id=1, source_target_pairs={{0,1},{1,0},{2,3},{3,2},{4,5},{5,4},{6,7},{7,6}} | collective-permute-start | bytes 6291464 | tf_op jit(solution)/shard_map/ppermute | solution.py:151
  187.3 29.4 %collective-permute-start.19 = (bf16[4,256,1024]{2,1,0:T(8,128)(2,1)}, bf16[4,256,1024]{2,1,0:T(8,128)(2,1)}, u32[]{:S(2)}, u32[]{:S(2)}) collective-permute-start(bf16[4,256,1024]{2,1,0:T(8,128)(2,1)} %collective-permute-done.15.refs_3_), channel_id=1, source_target_pairs={{0,1},{1,0},{2,3},{3,2},{4,5},{5,4},{6,7},{7,6}} | collective-permute-start | bytes 6291464 | tf_op jit(solution)/shard_map/ppermute | solution.py:151
  187.8 26.3 %collective-permute-start.20 = (bf16[2,256,1024]{2,1,0:T(8,128)(2,1)}, bf16[2,256,1024]{2,1,0:T(8,128)(2,1)}, u32[]{:S(2)}, u32[]{:S(2)}) collective-permute-start(bf16[2,256,1024]{2,1,0:T(8,128)(2,1)} %get-tuple-element.51.refs_3_), channel_id=1, source_target_pairs={{0,2},{1,3},{2,0},{3,1},{4,6},{5,7},{6,4},{7,5}} | collective-permute-start | bytes 3145736 | tf_op jit(solution)/shard_map/ppermute | solution.py:151
  189.3 26.9 %collective-permute-start.21 = (bf16[2,256,1024]{2,1,0:T(8,128)(2,1)}, bf16[2,256,1024]{2,1,0:T(8,128)(2,1)}, u32[]{:S(2)}, u32[]{:S(2)}) collective-permute-start(bf16[2,256,1024]{2,1,0:T(8,128)(2,1)} %get-tuple-element.50.refs_1_), channel_id=1, source_target_pairs={{0,4},{1,5},{2,6},{3,7},{4,0},{5,1},{6,2},{7,3}} | collective-permute-start | bytes 3145736 | tf_op jit(solution)/shard_map/ppermute | solution.py:151
  189.8 51.2 %collective-permute-start.12 = (bf16[2,256,1024]{2,1,0:T(8,128)(2,1)}, bf16[2,256,1024]{2,1,0:T(8,128)(2,1)}, u32[]{:S(2)}, u32[]{:S(2)}) collective-permute-start(bf16[2,256,1024]{2,1,0:T(8,128)(2,1)} %collective-permute-done.1.refs_3_), channel_id=1, source_target_pairs={{0,2},{1,3},{2,0},{3,1},{4,6},{5,7},{6,4},{7,5}} | collective-permute-start | bytes 3145736 | tf_op jit(solution)/shard_map/ppermute | solution.py:151
  214.1 26.8 %collective-permute-start.13 = (bf16[2,256,1024]{2,1,0:T(8,128)(2,1)}, bf16[2,256,1024]{2,1,0:T(8,128)(2,1)}, u32[]{:S(2)}, u32[]{:S(2)}) collective-permute-start(bf16[2,256,1024]{2,1,0:T(8,128)(2,1)} %collective-permute-done.refs_2_), channel_id=1, source_target_pairs={{0,4},{1,5},{2,6},{3,7},{4,0},{5,1},{6,2},{7,3}} | collective-permute-start | bytes 3145736 | tf_op jit(solution)/shard_map/ppermute | solution.py:151
  216.2 25.3 %collective-permute-start.26 = (bf16[2,256,1024]{2,1,0:T(8,128)(2,1)}, bf16[2,256,1024]{2,1,0:T(8,128)(2,1)}, u32[]{:S(2)}, u32[]{:S(2)}) collective-permute-start(bf16[2,256,1024]{2,1,0:T(8,128)(2,1)} %collective-permute-done.20.refs_2_), channel_id=1, source_target_pairs={{0,1},{1,0},{2,3},{3,2},{4,5},{5,4},{6,7},{7,6}} | collective-permute-start | bytes 3145736 | tf_op jit(solution)/shard_map/ppermute | solution.py:151
  216.2 25.3 %collective-permute-start.27 = (bf16[2,256,1024]{2,1,0:T(8,128)(2,1)}, bf16[2,256,1024]{2,1,0:T(8,128)(2,1)}, u32[]{:S(2)}, u32[]{:S(2)}) collective-permute-start(bf16[2,256,1024]{2,1,0:T(8,128)(2,1)} %collective-permute-done.21.refs_3_), channel_id=1, source_target_pairs={{0,1},{1,0},{2,3},{3,2},{4,5},{5,4},{6,7},{7,6}} | collective-permute-start | bytes 3145736 | tf_op jit(solution)/shard_map/ppermute | solution.py:151
  241.0 17.7 %collective-permute-start.24 = (bf16[2,256,1024]{2,1,0:T(8,128)(2,1)}, bf16[2,256,1024]{2,1,0:T(8,128)(2,1)}, u32[]{:S(2)}, u32[]{:S(2)}) collective-permute-start(bf16[2,256,1024]{2,1,0:T(8,128)(2,1)} %collective-permute-done.12.refs_2_), channel_id=1, source_target_pairs={{0,1},{1,0},{2,3},{3,2},{4,5},{5,4},{6,7},{7,6}} | collective-permute-start | bytes 3145736 | tf_op jit(solution)/shard_map/ppermute | solution.py:151
  241.0 17.7 %collective-permute-start.25 = (bf16[2,256,1024]{2,1,0:T(8,128)(2,1)}, bf16[2,256,1024]{2,1,0:T(8,128)(2,1)}, u32[]{:S(2)}, u32[]{:S(2)}) collective-permute-start(bf16[2,256,1024]{2,1,0:T(8,128)(2,1)} %collective-permute-done.13.refs_3_), channel_id=1, source_target_pairs={{0,1},{1,0},{2,3},{3,2},{4,5},{5,4},{6,7},{7,6}} | collective-permute-start | bytes 3145736 | tf_op jit(solution)/shard_map/ppermute | solution.py:151

commit v2 on v0

v2 whole, which is shorter than its diff:
```python
import functools

import jax
import jax.numpy as jnp
from jax import lax
from jax.experimental import pallas as pl
from jax.experimental.pallas import tpu as pltpu
from jax.sharding import PartitionSpec as P


NORM_EPS = 1e-6

CORE, NEAR_X, NEAR_Y, DIAGONAL = 1, 2, 4, 6
PIECES = (4, 2)
ORDER = ("a0", "b0", "f0", "a1", "b1", "f1")
JOINED = ("a0",)

HBM = pl.BlockSpec(memory_space=pltpu.HBM)
VMEM = pl.BlockSpec(memory_space=pltpu.VMEM)


def rms_norm(enc_out, norm_scale):
    acts = enc_out.astype(jnp.float32)
    mean_sq = jnp.mean(acts * acts, axis=-1, keepdims=True)
    return (acts * lax.rsqrt(mean_sq + NORM_EPS) * norm_scale.astype(jnp.float32)).astype(jnp.bfloat16)


def prepare_kernel(pieces, has_weights, *refs):
    enc_out, norm_scale, *refs = refs
    entries = [(p, e, first + e) for p, (first, n) in enumerate(pieces) for e in range(n)]
    if has_weights:
        w_in, refs = refs[:2], refs[2:]
    outs, refs = refs[: len(pieces)], refs[len(pieces) :]
    if has_weights:
        w_out, refs = refs[:2], refs[2:]
    x, y, scale, in_sem, out_sem, scale_sem, *refs = refs
    load_scale = pltpu.make_async_copy(norm_scale, scale, scale_sem)
    load_scale.start()
    loads = [pltpu.make_async_copy(enc_out.at[b], x.at[k], in_sem.at[k]) for k, (_, _, b) in enumerate(entries)]
    stores = [pltpu.make_async_copy(y.at[k], outs[p].at[e], out_sem.at[k]) for k, (p, e, _) in enumerate(entries)]
    for copy in loads:
        copy.start()
    w_loads = []
    if has_weights:
        w_raw, w_sem = refs
        n_layers = w_raw.shape[1]
        w_loads = [(i, l, pltpu.make_async_copy(w_in[i].at[l], w_raw.at[i, l], w_sem.at[i, l])) for l in range(n_layers) for i in (0, 1)]
    for _, _, copy in w_loads:
        copy.start()
    load_scale.wait()

    def normalize(k, _):
        pltpu.make_async_copy(enc_out.at[0], x.at[k], in_sem.at[k]).wait()
        y[k] = rms_norm(x[k], scale[...])
        for i, store in enumerate(stores):

            @pl.when(k == i)
            def _():
                store.start()

        return 0

    lax.fori_loop(0, len(entries), normalize, 0)
    if has_weights:

        def lay_out(l, _):
            for i in (0, 1):
                pltpu.make_async_copy(w_in[i].at[l], w_raw.at[i, l], w_sem.at[i, l]).wait()
                w_out[i][l] = w_raw[i, l].reshape(w_out[i].shape[1:])
            return 0

        lax.fori_loop(0, n_layers, lay_out, 0)
    for store in stores:
        store.wait()


def prepare(enc_out, norm_scale, pieces, weights=()):
    _, seq, width = enc_out.shape
    n = sum(n for _, n in pieces)
    out_shape = [jax.ShapeDtypeStruct((n, seq, width), jnp.bfloat16) for _, n in pieces]
    scratch = [pltpu.VMEM((n, seq, width), jnp.bfloat16)] * 2 + [pltpu.VMEM((width,), jnp.bfloat16)]
    scratch += [pltpu.SemaphoreType.DMA((n,))] * 2 + [pltpu.SemaphoreType.DMA]
    for w in weights[:1]:
        n_layers, _, heads, head_dim = w.shape
        out_shape += [jax.ShapeDtypeStruct((n_layers, width, heads * head_dim), jnp.bfloat16)] * 2
        scratch += [pltpu.VMEM((2, *w.shape), jnp.bfloat16), pltpu.SemaphoreType.DMA((2, n_layers))]
    return pl.pallas_call(
        functools.partial(prepare_kernel, pieces, bool(weights)),
        out_shape=out_shape,
        in_specs=[HBM] * (2 + len(weights)),
        out_specs=[HBM] * len(pieces) + [VMEM] * len(weights),
        scratch_shapes=scratch,
        compiler_params=pltpu.CompilerParams(vmem_limit_bytes=(32 if weights else 57) * 2**20),
        cost_estimate=pl.CostEstimate(flops=8 * n * seq * width, bytes_accessed=4 * n * seq * width, transcendentals=0),
    )(*[pltpu.with_memory_space_constraint(a, pltpu.HBM) for a in (enc_out, norm_scale, *weights)])


def together(*values):
    return lax.optimization_barrier(values)


def pick(n, values):
    out = values[-1]
    for k in range(len(values) - 2, -1, -1):
        out = jnp.where(n == k, values[k], out)
    return out


def multiply_unit(x, weights, rounded, slot, stores):
    for j in range(rounded.shape[1]):
        product = jnp.dot(x, weights[j % 2][j // 2], preferred_element_type=jnp.float32)
        rounded[slot, j] = product.reshape(rounded.shape[2:]).astype(jnp.bfloat16)
        for copy in stores([j]):
            copy.start()


def unit_stores(rounded, outs, sem, slot, places, matrices):
    rows = rounded.shape[2] // len(places)
    for g, (entry, source) in enumerate(places):
        for j in matrices:
            to = outs[j % 2].at[j // 2, entry, pl.ds(pl.multiple_of(source * rows, rows), rows)]
            yield pltpu.make_async_copy(rounded.at[slot, j, pl.ds(g * rows, rows)], to, sem.at[slot, j, g])


def run_units(n_units, prefetch, tokens, weights, outs, rounded, sem, places):
    every = range(rounded.shape[1])

    def body(n, _):
        slot = lax.rem(n, 2)
        prefetch(n, slot)

        @pl.when(n >= 2)
        def _():
            for copy in unit_stores(rounded, outs, sem, slot, places(n), every):
                copy.wait()

        multiply_unit(tokens(n, slot), weights, rounded, slot, lambda js: unit_stores(rounded, outs, sem, slot, places(n), js))
        return 0

    lax.fori_loop(0, n_units, body, 0)
    for n in range(max(n_units - 2, 0), n_units):
        for copy in unit_stores(rounded, outs, sem, n % 2, places(n), every):
            copy.wait()


def project_hbm_kernel(plan, *refs):
    arrays, weights = refs[: len(plan)], refs[len(plan) : len(plan) + 2]
    *outs, rounded, out_sem, rows, in_sem = refs[-6:]
    seq = arrays[0].shape[1]
    me = lax.axis_index("tp")
    flat = [(a, e, first + e, mask) for a, (n, first, mask) in enumerate(plan) for e in range(n)]
    units = [flat[k : k + 2] for k in range(0, len(flat), 2)]

    def load(n, slot):
        for k, unit in enumerate(units):

            @pl.when(n == k)
            def _():
                for g, (a, e, _, _) in enumerate(unit):
                    pltpu.make_async_copy(arrays[a].at[e], rows.at[slot, pl.ds(g * seq, seq)], in_sem.at[slot, g]).start()

    def prefetch(n, slot):
        for g in range(2):
            pltpu.make_async_copy(arrays[0].at[0], rows.at[slot, pl.ds(g * seq, seq)], in_sem.at[slot, g]).wait()

        @pl.when(n + 1 < len(units))
        def _():
            load(n + 1, 1 - slot)

    def places(n):
        return [(pick(n, [u[g][2] for u in units]), me ^ pick(n, [u[g][3] for u in units])) for g in range(2)]

    load(0, 0)
    run_units(len(units), prefetch, lambda n, slot: rows[slot], weights, outs, rounded, out_sem, places)


def project_vmem_kernel(plan, *refs):
    arrays, weights = refs[: len(plan)], refs[len(plan) : len(plan) + 2]
    *outs, rounded, out_sem = refs[-4:]
    me = lax.axis_index("tp")
    run_units(
        plan[0][0],
        lambda n, slot: None,
        lambda n, slot: jnp.concatenate([a[n] for a in arrays], axis=0),
        weights,
        outs,
        rounded,
        out_sem,
        lambda n: [(first + n, me ^ mask) for _, first, mask in plan],
    )


def project(in_vmem, vmem_mib, arrays, plan, weights, caches, cache_shape):
    n_arrays = len(arrays)
    n_layers, width, columns = weights[0].shape
    seq = arrays[0].shape[1]
    entries = sum(n for n, _, _ in plan)
    if in_vmem:
        arrays = [pltpu.with_memory_space_constraint(a, pltpu.VMEM) for a in arrays]
    elif caches:
        arrays = [pltpu.with_memory_space_constraint(a, pltpu.HBM) for a in arrays]
    weights = [pltpu.with_memory_space_constraint(w, pltpu.VMEM) for w in weights]
    scratch = [pltpu.VMEM((2, 2 * n_layers, 2 * seq * columns // 128, 128), jnp.bfloat16), pltpu.SemaphoreType.DMA((2, 2 * n_layers, 2))]
    if not in_vmem:
        scratch += [pltpu.VMEM((2, 2 * seq, width), jnp.bfloat16), pltpu.SemaphoreType.DMA((2, 2))]
    return pl.pallas_call(
        functools.partial(project_vmem_kernel if in_vmem else project_hbm_kernel, plan),
        out_shape=[jax.ShapeDtypeStruct(cache_shape, jnp.bfloat16)] * 2,
        in_specs=[VMEM if in_vmem else HBM] * n_arrays + [VMEM, VMEM] + [HBM] * len(caches),
        out_specs=[HBM, HBM],
        input_output_aliases={n_arrays + 2 + i: i for i in range(len(caches))},
        scratch_shapes=scratch,
        compiler_params=pltpu.CompilerParams(vmem_limit_bytes=vmem_mib * 2**20),
        cost_estimate=pl.CostEstimate(
            flops=2 * entries * seq * width * columns * 2 * n_layers,
            bytes_accessed=2 * entries * seq * (width + columns * 2 * n_layers),
            transcendentals=0,
        ),
    )(*arrays, *weights, *caches)


def solution(mesh):
    def per_device(enc_out, norm_scale, w_key, w_value):
        n_batch, seq, _ = enc_out.shape
        n_layers, _, heads, head_dim = w_key.shape
        n_dev = mesh.shape["tp"]

        def swap(a, mask):
            return lax.ppermute(a, "tp", [(i, i ^ mask) for i in range(n_dev)])

        first = [sum(PIECES[:k]) for k in range(len(PIECES))]
        half = sum(PIECES)
        spans = [[(n, s * half + f) for f, n in zip(first, PIECES)] for s in (0, 1)]
        own = [list(ys) for ys in zip(prepare(enc_out, norm_scale, [(spans[s][0][1], PIECES[0]) for s in (0, 1)]))]
        rest = [(spans[s][k][1], n) for k, n in enumerate(PIECES) if k for s in (0, 1)]
        own[0][0], own[1][0], enc_out = together(own[0][0], own[1][0], enc_out)
        *ys, w_key, w_value = prepare(enc_out, norm_scale, rest, (w_key, w_value))
        weights = [w_key, w_value]
        for k in range(len(rest) // 2):
            for s in (0, 1):
                own[s].append(ys[2 * k + s])

        arrived = {}

        def send(what):
            for link, mask in ((0, NEAR_X), (1, NEAR_Y)):
                kind, k = what[0], int(what[1])
                if kind == "f":
                    array, span, _ = arrived[1 - link, f"a{k}"]
                    arrived[link, what] = [swap(array, mask), span, DIAGONAL]
                else:
                    s = link if kind == "a" else 1 - link
                    arrived[link, what] = [swap(own[s][k], mask), spans[s][k], mask]

        def to_partner(group):
            return [[swap(a, CORE), span, mask ^ CORE] for a, span, mask in group]

        for what in ORDER:
            if what[0] != "f":
                send(what)
        mine = [[own[s][k], spans[s][k], 0] for k in range(len(PIECES)) for s in (0, 1)]
        theirs = to_partner(mine)
        cache_shape = (n_layers, n_batch, n_dev * seq * heads, head_dim)

        def call(in_vmem, vmem_mib, group, caches):
            return project(in_vmem, vmem_mib, [a for a, _, _ in group], [(*span, mask) for _, span, mask in group], weights, caches, cache_shape)

        caches = call(False, 57, mine + theirs, ())
        left = []
        for what in ORDER:
            group = [arrived[link, what] for link in (0, 1)]
            group[0][0], group[1][0], *caches = together(group[0][0], group[1][0], *caches)
            if what[0] == "a":
                send("f" + what[1])
            swapped = to_partner(group)
            caches = call(False, 24, left + group, caches)
            left = swapped if what in JOINED else []
            if not left:
                caches = call(True, 24, swapped, caches)
        return tuple(c.reshape(n_layers, n_batch, n_dev * seq, heads, head_dim) for c in caches)

    weight_spec = P(None, None, "tp", None)
    cache_spec = P(None, "dp", None, "tp", None)
    return jax.shard_map(per_device, mesh=mesh, in_specs=(P("dp", "tp", None), P(None), weight_spec, weight_spec), out_specs=(cache_spec, cache_spec), check_vma=False)
```

time: 624 us -> 266 us (0.43)
  Pallas kernels: 0 us -> 201 us
  waiting for transfers between devices: 230 us -> 37.4 us
  local copies, waits for them, and re-layouts: 195 us -> 3.69 us
  matrix products: 173 us -> 0 us
  starting transfers between devices: 0.04 us -> 22.3 us
  between operations: 14 us -> 1.2 us
  other arithmetic: 12.1 us -> 0 us
    all_gather x1 -> x0, waiting for transfers between devices: 230 us -> none  [per_device(): gathered = lax.all_gather(normed, 'tp', axis=1, tiled=True)]
    pallas_call x0 -> x14, Pallas kernels: none -> 201 us  [the longest x12 190 us: project(): pl.pallas_call(functools.partial(project_vmem_kernel if in_vmem else proj...]
    unnamed x6 -> x36, local copies, waits for them, and re-layouts: 195 us -> 3.69 us
    dot_general x2 -> x0, matrix products: 173 us -> none  [the longest x1 86.5 us: per_device(): jnp.einsum('bsd,ldhk->lbshk', gathered, w_value, preferred_element_type=j...]
    ppermute x0 -> x28, waiting for transfers between devices: none -> 37.4 us  [swap(): return lax.ppermute(a, 'tp', [(i, i ^ mask) for i in range(n_dev)])]
    ppermute x0 -> x28, starting transfers between devices: none -> 22.3 us  [swap(): return lax.ppermute(a, 'tp', [(i, i ^ mask) for i in range(n_dev)])]
    convert_element_type x2 -> x0, other arithmetic: 7.84 us -> none  [the longest x1 7.15 us: rms_norm(): (acts * lax.rsqrt(mean_sq + NORM_EPS) * norm_scale.astype(jnp.float32)).a...]
  transfers between devices with their start and end apart: 1 -> 28, of which waited for: 1 -> 5; matrix products, arithmetic and copies ran while one was open for 0% -> 0% of each run, Pallas kernels for 0% -> 71%
where the time goes in v2:
time: 266 us
  Pallas kernels  201 us (76%)
  waiting for transfers between devices  37.4 us (14%)
  starting transfers between devices  22.3 us (8%)
  local copies, waits for them, and re-layouts  3.69 us (1%)
    pallas_call x12, Pallas kernels, project(): pl.pallas_call(functools.partial(project_vmem_kernel if in_vmem else proj...  190 us
    ppermute x28, waiting for transfers between devices, swap(): return lax.ppermute(a, 'tp', [(i, i ^ mask) for i in range(n_dev)])  37.4 us
    ppermute x28, starting transfers between devices, swap(): return lax.ppermute(a, 'tp', [(i, i ^ mask) for i in range(n_dev)])  22.3 us
    pallas_call x2, Pallas kernels, prepare(): pl.pallas_call(functools.partial(prepare_kernel, pieces, bool(weights)),...  11.4 us
  transfers between devices with their start and end apart: 28, of which 5 were waited for; matrix products, arithmetic and copies ran while one was open for 0% of the time, Pallas kernels for 71%

profile of v2, /device:TPU:0, one launch (start us, length us, event | category | flops | bytes accessed | tf_op | source)
XLA Modules:
  0.0 265.9 jit_solution(6932391701300765539)
XLA Ops:
  0.6 4.5 %shard_map.59 = (bf16[4,256,1024]{2,1,0:T(8,128)(2,1)}, bf16[4,256,1024]{2,1,0:T(8,128)(2,1)}) custom-call(bf16[12,256,1024]{2,1,0:T(8,128)(2,1)} %refs_0_.2, bf16[1024]{0:T(1024)(128)(2,1)} %refs_1_.3), custom_call_target="tpu_custom_call" | custom-call | flops 16777216 | bytes 8388608 | tf_op jit(solution)/shard_map/pallas_call | solution.py:87
  5.1 0.9 collective-permute-start.4
  6.0 0.0 collective-permute-start.5
  6.0 7.0 %shard_map.60 = (bf16[2,256,1024]{2,1,0:T(8,128)(2,1)S(1)}, bf16[2,256,1024]{2,1,0:T(8,128)(2,1)S(1)}, bf16[3,1024,512]{2,1,0:T(8,128)(2,1)S(1)}, bf16[3,1024,512]{2,1,0:T(8,128)(2,1)S(1)}) custom-call(bf16[12,256,1024]{2,1,0:T(8,128)(2,1)} %refs_0_.2, bf16[1024]{0:T(1024)(128)(2,1)} %refs_1_.3, bf16[3,1024,4,128]{3,2,1,0:T(4,128)(2,1)} %refs_2_.1, ...), custom_call_target="tpu_custom_call" | custom-call | flops 8388608 | bytes 4194304 | tf_op jit(solution)/shard_map/pallas_call | solution.py:87
  13.0 1.0 copy-done
  13.9 0.5 collective-permute-start.6
  14.4 0.0 collective-permute-start.7
  14.5 2.9 %collective-permute-start.2 = (bf16[4,256,1024]{2,1,0:T(8,128)(2,1)}, bf16[4,256,1024]{2,1,0:T(8,128)(2,1)}, u32[]{:S(2)}, u32[]{:S(2)}) collective-permute-start(bf16[4,256,1024]{2,1,0:T(8,128)(2,1)} %get-tuple-element.64.refs_0_), channel_id=1, source_target_pairs={{0,2},{1,3},{2,0},{3,1},{4,6},{5,7},{6,4},{7,5}} | collective-permute-start | bytes 6291464 | tf_op jit(solution)/shard_map/ppermute | solution.py:229
  17.4 0.0 collective-permute-done.6.refs_6_
  17.4 2.2 collective-permute-start.3
  19.6 0.0 collective-permute-done.7.refs_7_
  19.6 1.5 collective-permute-start.10
  21.1 0.0 collective-permute-done.4.refs_4_
  21.1 1.5 collective-permute-start.11
  22.6 0.0 collective-permute-done.5.refs_5_
  22.6 44.6 %shard_map.61 = (bf16[3,12,8192,128]{3,2,1,0:T(8,128)(2,1)}, bf16[3,12,8192,128]{3,2,1,0:T(8,128)(2,1)}) custom-call(bf16[4,256,1024]{2,1,0:T(8,128)(2,1)} %get-tuple-element.64.refs_0_, bf16[4,256,1024]{2,1,0:T(8,128)(2,1)} %get-tuple-element.65.refs_1_, bf16[2,256,1024]{2,1,0:T(8,128)(2,1)} %copy-done, bf16[2,256,1024]{2,1,0:T(8,128)(2,1)} %copy-done.2, ...), custom_call_target="tpu_custom_call" | custom-call | flops 38654705664 | bytes 50331648 | tf_op jit(solution)/shard_map/pallas_call | solution.py:206
  67.2 0.0 collective-permute-done.2.refs_0_
  67.2 0.0 collective-permute-done.3.refs_1_
  67.2 0.0 collective-permute-start.14
  67.2 0.5 collective-permute-start.15
  67.7 1.1 collective-permute-start.8
  68.9 16.3 %shard_map.62 = (bf16[3,12,8192,128]{3,2,1,0:T(8,128)(2,1)}, bf16[3,12,8192,128]{3,2,1,0:T(8,128)(2,1)}) custom-call(bf16[4,256,1024]{2,1,0:T(8,128)(2,1)} %collective-permute-done.2.refs_0_, bf16[4,256,1024]{2,1,0:T(8,128)(2,1)} %collective-permute-done.3.refs_1_, ...), custom_call_target="tpu_custom_call", output_to_operand_aliasing={{0}: (4, {}), {1}: (5, {})} | custom-call | flops 12884901888 | bytes 16777216 | tf_op jit(solution)/shard_map/pallas_call | solution.py:206
  85.2 24.0 %collective-permute-done.10.refs_2_ = bf16[4,256,1024]{2,1,0:T(8,128)(2,1)} collective-permute-done((bf16[4,256,1024]{2,1,0:T(8,128)(2,1)}, bf16[4,256,1024]{2,1,0:T(8,128)(2,1)}, u32[]{:S(2)}, u32[]{:S(2)}) %collective-permute-start.10) | collective-permute-done | bytes 2097184 | tf_op jit(solution)/shard_map/ppermute | solution.py:229
  109.1 2.1 collective-permute-start.9
  111.2 0.0 collective-permute-done.14.refs_0_
  111.2 0.5 collective-permute-start.13
  111.7 0.0 collective-permute-done.15.refs_1_
  111.7 0.8 copy-done.6
  112.6 1.3 copy-done.7
  113.9 30.4 %shard_map.63 = (bf16[3,12,8192,128]{3,2,1,0:T(8,128)(2,1)}, bf16[3,12,8192,128]{3,2,1,0:T(8,128)(2,1)}) custom-call(bf16[4,256,1024]{2,1,0:T(8,128)(2,1)} %copy-done.6, bf16[4,256,1024]{2,1,0:T(8,128)(2,1)} %copy-done.7, bf16[4,256,1024]{2,1,0:T(8,128)(2,1)} %collective-permute-done.10.refs_2_, ...), custom_call_target="tpu_custom_call", output_to_operand_aliasing={{0}: (6, {}), {1}: (7, {})} | custom-call | flops 25769803776 | bytes 33554432 | tf_op jit(solution)/shard_map/pallas_call | solution.py:206
  144.4 15.2 %shard_map.64 = (bf16[3,12,8192,128]{3,2,1,0:T(8,128)(2,1)}, bf16[3,12,8192,128]{3,2,1,0:T(8,128)(2,1)}) custom-call(bf16[4,256,1024]{2,1,0:T(8,128)(2,1)S(1)} %collective-permute-done.12.refs_0_, bf16[4,256,1024]{2,1,0:T(8,128)(2,1)S(1)} %collective-permute-done.13.refs_1_, ...), custom_call_target="tpu_custom_call", output_to_operand_aliasing={{0}: (4, {}), {1}: (5, {})} | custom-call | flops 12884901888 | bytes 16777216 | tf_op jit(solution)/shard_map/pallas_call | solution.py:206
  159.6 0.0 collective-permute-done.8.refs_0_
  159.6 0.0 collective-permute-done.9.refs_1_
  159.6 0.5 collective-permute-start.16
  160.2 0.0 collective-permute-start.17
  160.2 1.5 collective-permute-start
  161.7 1.5 collective-permute-start.1
  163.2 16.3 %shard_map.65 = (bf16[3,12,8192,128]{3,2,1,0:T(8,128)(2,1)}, bf16[3,12,8192,128]{3,2,1,0:T(8,128)(2,1)}) custom-call(bf16[4,256,1024]{2,1,0:T(8,128)(2,1)} %copy-done.4, bf16[4,256,1024]{2,1,0:T(8,128)(2,1)} %copy-done.5, bf16[3,1024,512]{2,1,0:T(8,128)(2,1)S(1)} %get-tuple-element.66.refs_8_.refs_2_.refs_4_, ...), custom_call_target="tpu_custom_call", output_to_operand_aliasing={{0}: (4, {}), {1}: (5, {})} | custom-call | flops 12884901888 | bytes 16777216 | tf_op jit(solution)/shard_map/pallas_call | solution.py:206
  179.5 15.0 %shard_map.66 = (bf16[3,12,8192,128]{3,2,1,0:T(8,128)(2,1)}, bf16[3,12,8192,128]{3,2,1,0:T(8,128)(2,1)}) custom-call(bf16[4,256,1024]{2,1,0:T(8,128)(2,1)S(1)} %collective-permute-done.16.refs_0_, bf16[4,256,1024]{2,1,0:T(8,128)(2,1)S(1)} %collective-permute-done.17.refs_1_, ...), custom_call_target="tpu_custom_call", output_to_operand_aliasing={{0}: (4, {}), {1}: (5, {})} | custom-call | flops 12884901888 | bytes 16777216 | tf_op jit(solution)/shard_map/pallas_call | solution.py:206
  194.5 0.0 collective-permute-done.1.refs_1_
  194.6 0.0 collective-permute-start.22
  194.6 0.5 collective-permute-start.23
  195.1 0.5 collective-permute-start.20
  195.6 0.9 collective-permute-start.21
  196.5 9.2 %shard_map.67 = (bf16[3,12,8192,128]{3,2,1,0:T(8,128)(2,1)}, bf16[3,12,8192,128]{3,2,1,0:T(8,128)(2,1)}) custom-call(bf16[2,256,1024]{2,1,0:T(8,128)(2,1)} %copy-done.8, bf16[2,256,1024]{2,1,0:T(8,128)(2,1)} %copy-done.10, bf16[3,1024,512]{2,1,0:T(8,128)(2,1)S(1)} %get-tuple-element.66.refs_8_.refs_2_.refs_4_, ...), custom_call_target="tpu_custom_call", output_to_operand_aliasing={{0}: (4, {}), {1}: (5, {})} | custom-call | flops 6442450944 | bytes 8388608 | tf_op jit(solution)/shard_map/pallas_call | solution.py:206
  205.8 0.0 collective-permute-done.22.refs_0_
  205.8 8.2 %shard_map.68 = (bf16[3,12,8192,128]{3,2,1,0:T(8,128)(2,1)}, bf16[3,12,8192,128]{3,2,1,0:T(8,128)(2,1)}) custom-call(bf16[2,256,1024]{2,1,0:T(8,128)(2,1)S(1)} %collective-permute-done.22.refs_0_, bf16[2,256,1024]{2,1,0:T(8,128)(2,1)S(1)} %collective-permute-done.23.refs_1_, ...), custom_call_target="tpu_custom_call", output_to_operand_aliasing={{0}: (4, {}), {1}: (5, {})} | custom-call | flops 6442450944 | bytes 8388608 | tf_op jit(solution)/shard_map/pallas_call | solution.py:206
  214.0 6.1 %collective-permute-done.20.refs_0_ = bf16[2,256,1024]{2,1,0:T(8,128)(2,1)S(1)} collective-permute-done((bf16[2,256,1024]{2,1,0:T(8,128)(2,1)S(1)}, bf16[2,256,1024]{2,1,0:T(8,128)(2,1)S(1)}, u32[]{:S(2)}, u32[]{:S(2)}) %collective-permute-start.20) | collective-permute-done | bytes 1048608 | tf_op jit(solution)/shard_map/ppermute | solution.py:229
  220.2 0.3 collective-permute-done.21.refs_1_
  220.4 0.0 collective-permute-start.24
  220.4 0.5 collective-permute-start.25
  221.0 1.5 collective-permute-start.18
  222.4 0.5 collective-permute-start.19
  223.0 9.2 %shard_map.69 = (bf16[3,12,8192,128]{3,2,1,0:T(8,128)(2,1)}, bf16[3,12,8192,128]{3,2,1,0:T(8,128)(2,1)}) custom-call(bf16[2,256,1024]{2,1,0:T(8,128)(2,1)} %copy-done.12, bf16[2,256,1024]{2,1,0:T(8,128)(2,1)} %copy-done.13, bf16[3,1024,512]{2,1,0:T(8,128)(2,1)S(1)} %get-tuple-element.66.refs_8_.refs_2_.refs_4_, ...), custom_call_target="tpu_custom_call", output_to_operand_aliasing={{0}: (4, {}), {1}: (5, {})} | custom-call | flops 6442450944 | bytes 8388608 | tf_op jit(solution)/shard_map/pallas_call | solution.py:206
  232.2 0.0 collective-permute-done.25.refs_1_
  232.3 8.0 %shard_map.70 = (bf16[3,12,8192,128]{3,2,1,0:T(8,128)(2,1)}, bf16[3,12,8192,128]{3,2,1,0:T(8,128)(2,1)}) custom-call(bf16[2,256,1024]{2,1,0:T(8,128)(2,1)S(1)} %collective-permute-done.24.refs_0_, bf16[2,256,1024]{2,1,0:T(8,128)(2,1)S(1)} %collective-permute-done.25.refs_1_, ...), custom_call_target="tpu_custom_call", output_to_operand_aliasing={{0}: (4, {}), {1}: (5, {})} | custom-call | flops 6442450944 | bytes 8388608 | tf_op jit(solution)/shard_map/pallas_call | solution.py:206
  240.3 5.7 %collective-permute-done.18.refs_0_ = bf16[2,256,1024]{2,1,0:T(8,128)(2,1)S(1)} collective-permute-done((bf16[2,256,1024]{2,1,0:T(8,128)(2,1)S(1)}, bf16[2,256,1024]{2,1,0:T(8,128)(2,1)S(1)}, u32[]{:S(2)}, u32[]{:S(2)}) %collective-permute-start.18) | collective-permute-done | bytes 1048608 | tf_op jit(solution)/shard_map/ppermute | solution.py:229
  246.0 1.2 collective-permute-done.19.refs_1_
  247.2 0.0 collective-permute-start.26
  247.2 0.5 collective-permute-start.27
  247.8 0.5 copy-done.15
  248.2 9.2 %shard_map.71 = (bf16[3,12,8192,128]{3,2,1,0:T(8,128)(2,1)}, bf16[3,12,8192,128]{3,2,1,0:T(8,128)(2,1)}) custom-call(bf16[2,256,1024]{2,1,0:T(8,128)(2,1)} %copy-done.14, bf16[2,256,1024]{2,1,0:T(8,128)(2,1)} %copy-done.15, bf16[3,1024,512]{2,1,0:T(8,128)(2,1)S(1)} %get-tuple-element.66.refs_8_.refs_2_.refs_4_, ...), custom_call_target="tpu_custom_call", output_to_operand_aliasing={{0}: (4, {}), {1}: (5, {})} | custom-call | flops 6442450944 | bytes 8388608 | tf_op jit(solution)/shard_map/pallas_call | solution.py:206
  257.5 0.0 collective-permute-done.26.refs_0_
  257.5 8.3 %shard_map.72 = (bf16[3,12,8192,128]{3,2,1,0:T(8,128)(2,1)}, bf16[3,12,8192,128]{3,2,1,0:T(8,128)(2,1)}) custom-call(bf16[2,256,1024]{2,1,0:T(8,128)(2,1)S(1)} %collective-permute-done.26.refs_0_, bf16[2,256,1024]{2,1,0:T(8,128)(2,1)S(1)} %collective-permute-done.27.refs_1_, ...), custom_call_target="tpu_custom_call", output_to_operand_aliasing={{0}: (4, {}), {1}: (5, {})} | custom-call | flops 6442450944 | bytes 8388608 | tf_op jit(solution)/shard_map/pallas_call | solution.py:206
  (42 shorter events, 0.1 us)
Async XLA Ops:
  5.1 16.0 %collective-permute-start.4 = (bf16[4,256,1024]{2,1,0:T(8,128)(2,1)}, bf16[4,256,1024]{2,1,0:T(8,128)(2,1)}, u32[]{:S(2)}, u32[]{:S(2)}) collective-permute-start(bf16[4,256,1024]{2,1,0:T(8,128)(2,1)} %get-tuple-element.64.refs_0_), channel_id=1, source_target_pairs={{0,1},{1,0},{2,3},{3,2},{4,5},{5,4},{6,7},{7,6}} | collective-permute-start | bytes 6291464 | tf_op jit(solution)/shard_map/ppermute | solution.py:229
  6.0 16.6 %collective-permute-start.5 = (bf16[4,256,1024]{2,1,0:T(8,128)(2,1)}, bf16[4,256,1024]{2,1,0:T(8,128)(2,1)}, u32[]{:S(2)}, u32[]{:S(2)}) collective-permute-start(bf16[4,256,1024]{2,1,0:T(8,128)(2,1)} %get-tuple-element.65.refs_1_), channel_id=1, source_target_pairs={{0,1},{1,0},{2,3},{3,2},{4,5},{5,4},{6,7},{7,6}} | collective-permute-start | bytes 6291464 | tf_op jit(solution)/shard_map/ppermute | solution.py:229
  13.0 1.0 copy-start
  13.0 4.4 %copy-start.2 = (bf16[2,256,1024]{2,1,0:T(8,128)(2,1)}, bf16[2,256,1024]{2,1,0:T(8,128)(2,1)S(1)}, u32[]{:S(2)}) copy-start(bf16[2,256,1024]{2,1,0:T(8,128)(2,1)S(1)} %get-tuple-element.63.refs_3_) | copy-start | bytes 3145732
  13.9 3.5 %collective-permute-start.6 = (bf16[2,256,1024]{2,1,0:T(8,128)(2,1)S(1)}, bf16[2,256,1024]{2,1,0:T(8,128)(2,1)S(1)}, u32[]{:S(2)}, u32[]{:S(2)}) collective-permute-start(bf16[2,256,1024]{2,1,0:T(8,128)(2,1)S(1)} %get-tuple-element.62.refs_2_), channel_id=1, source_target_pairs={{0,1},{1,0},{2,3},{3,2},{4,5},{5,4},{6,7},{7,6}} | collective-permute-start | bytes 3145736 | tf_op jit(solution)/shard_map/ppermute | solution.py:229
  14.4 5.2 %collective-permute-start.7 = (bf16[2,256,1024]{2,1,0:T(8,128)(2,1)S(1)}, bf16[2,256,1024]{2,1,0:T(8,128)(2,1)S(1)}, u32[]{:S(2)}, u32[]{:S(2)}) collective-permute-start(bf16[2,256,1024]{2,1,0:T(8,128)(2,1)S(1)} %get-tuple-element.63.refs_3_), channel_id=1, source_target_pairs={{0,1},{1,0},{2,3},{3,2},{4,5},{5,4},{6,7},{7,6}} | collective-permute-start | bytes 3145736 | tf_op jit(solution)/shard_map/ppermute | solution.py:229
  14.5 52.7 %collective-permute-start.2 = (bf16[4,256,1024]{2,1,0:T(8,128)(2,1)}, bf16[4,256,1024]{2,1,0:T(8,128)(2,1)}, u32[]{:S(2)}, u32[]{:S(2)}) collective-permute-start(bf16[4,256,1024]{2,1,0:T(8,128)(2,1)} %get-tuple-element.64.refs_0_), channel_id=1, source_target_pairs={{0,2},{1,3},{2,0},{3,1},{4,6},{5,7},{6,4},{7,5}} | collective-permute-start | bytes 6291464 | tf_op jit(solution)/shard_map/ppermute | solution.py:229
  17.4 2.2 copy-start.16
  17.4 49.8 %collective-permute-start.3 = (bf16[4,256,1024]{2,1,0:T(8,128)(2,1)}, bf16[4,256,1024]{2,1,0:T(8,128)(2,1)}, u32[]{:S(2)}, u32[]{:S(2)}) collective-permute-start(bf16[4,256,1024]{2,1,0:T(8,128)(2,1)} %get-tuple-element.65.refs_1_), channel_id=1, source_target_pairs={{0,4},{1,5},{2,6},{3,7},{4,0},{5,1},{6,2},{7,3}} | collective-permute-start | bytes 6291464 | tf_op jit(solution)/shard_map/ppermute | solution.py:229
  19.6 1.5 copy-start.17
  19.6 89.5 %collective-permute-start.10 = (bf16[4,256,1024]{2,1,0:T(8,128)(2,1)}, bf16[4,256,1024]{2,1,0:T(8,128)(2,1)}, u32[]{:S(2)}, u32[]{:S(2)}) collective-permute-start(bf16[4,256,1024]{2,1,0:T(8,128)(2,1)} %get-tuple-element.65.refs_1_), channel_id=1, source_target_pairs={{0,2},{1,3},{2,0},{3,1},{4,6},{5,7},{6,4},{7,5}} | collective-permute-start | bytes 6291464 | tf_op jit(solution)/shard_map/ppermute | solution.py:229
  21.1 90.1 %collective-permute-start.11 = (bf16[4,256,1024]{2,1,0:T(8,128)(2,1)}, bf16[4,256,1024]{2,1,0:T(8,128)(2,1)}, u32[]{:S(2)}, u32[]{:S(2)}) collective-permute-start(bf16[4,256,1024]{2,1,0:T(8,128)(2,1)} %get-tuple-element.64.refs_0_), channel_id=1, source_target_pairs={{0,4},{1,5},{2,6},{3,7},{4,0},{5,1},{6,2},{7,3}} | collective-permute-start | bytes 6291464 | tf_op jit(solution)/shard_map/ppermute | solution.py:229
  67.2 44.0 %collective-permute-start.14 = (bf16[4,256,1024]{2,1,0:T(8,128)(2,1)}, bf16[4,256,1024]{2,1,0:T(8,128)(2,1)S(1)}, u32[]{:S(2)}, u32[]{:S(2)}) collective-permute-start(bf16[4,256,1024]{2,1,0:T(8,128)(2,1)} %collective-permute-done.2.refs_0_), channel_id=1, source_target_pairs={{0,1},{1,0},{2,3},{3,2},{4,5},{5,4},{6,7},{7,6}} | collective-permute-start | bytes 6291464 | tf_op jit(solution)/shard_map/ppermute | solution.py:229
  67.2 44.5 %collective-permute-start.15 = (bf16[4,256,1024]{2,1,0:T(8,128)(2,1)}, bf16[4,256,1024]{2,1,0:T(8,128)(2,1)S(1)}, u32[]{:S(2)}, u32[]{:S(2)}) collective-permute-start(bf16[4,256,1024]{2,1,0:T(8,128)(2,1)} %collective-permute-done.3.refs_1_), channel_id=1, source_target_pairs={{0,1},{1,0},{2,3},{3,2},{4,5},{5,4},{6,7},{7,6}} | collective-permute-start | bytes 6291464 | tf_op jit(solution)/shard_map/ppermute | solution.py:229
  67.7 91.8 %collective-permute-start.8 = (bf16[4,256,1024]{2,1,0:T(8,128)(2,1)}, bf16[4,256,1024]{2,1,0:T(8,128)(2,1)S(1)}, u32[]{:S(2)}, u32[]{:S(2)}) collective-permute-start(bf16[4,256,1024]{2,1,0:T(8,128)(2,1)} %collective-permute-done.3.refs_1_), channel_id=1, source_target_pairs={{0,2},{1,3},{2,0},{3,1},{4,6},{5,7},{6,4},{7,5}} | collective-permute-start | bytes 6291464 | tf_op jit(solution)/shard_map/ppermute | solution.py:229
  109.1 50.5 %collective-permute-start.9 = (bf16[4,256,1024]{2,1,0:T(8,128)(2,1)}, bf16[4,256,1024]{2,1,0:T(8,128)(2,1)S(1)}, u32[]{:S(2)}, u32[]{:S(2)}) collective-permute-start(bf16[4,256,1024]{2,1,0:T(8,128)(2,1)} %collective-permute-done.2.refs_0_), channel_id=1, source_target_pairs={{0,4},{1,5},{2,6},{3,7},{4,0},{5,1},{6,2},{7,3}} | collective-permute-start | bytes 6291464 | tf_op jit(solution)/shard_map/ppermute | solution.py:229
  111.2 33.1 %collective-permute-start.12 = (bf16[4,256,1024]{2,1,0:T(8,128)(2,1)}, bf16[4,256,1024]{2,1,0:T(8,128)(2,1)S(1)}, u32[]{:S(2)}, u32[]{:S(2)}) collective-permute-start(bf16[4,256,1024]{2,1,0:T(8,128)(2,1)} %collective-permute-done.10.refs_2_), channel_id=1, source_target_pairs={{0,1},{1,0},{2,3},{3,2},{4,5},{5,4},{6,7},{7,6}} | collective-permute-start | bytes 6291464 | tf_op jit(solution)/shard_map/ppermute | solution.py:229
  111.2 1.4 copy-start.6
  111.2 33.1 %collective-permute-start.13 = (bf16[4,256,1024]{2,1,0:T(8,128)(2,1)}, bf16[4,256,1024]{2,1,0:T(8,128)(2,1)S(1)}, u32[]{:S(2)}, u32[]{:S(2)}) collective-permute-start(bf16[4,256,1024]{2,1,0:T(8,128)(2,1)} %collective-permute-done.11.refs_3_), channel_id=1, source_target_pairs={{0,1},{1,0},{2,3},{3,2},{4,5},{5,4},{6,7},{7,6}} | collective-permute-start | bytes 6291464 | tf_op jit(solution)/shard_map/ppermute | solution.py:229
  112.6 1.3 copy-start.7
  144.4 15.8 %copy-start.1 = (bf16[2,256,1024]{2,1,0:T(8,128)(2,1)S(1)}, bf16[2,256,1024]{2,1,0:T(8,128)(2,1)}, u32[]{:S(2)}) copy-start(bf16[2,256,1024]{2,1,0:T(8,128)(2,1)} %copy-done) | copy-start | bytes 3145732
  144.4 17.3 %copy-start.3 = (bf16[2,256,1024]{2,1,0:T(8,128)(2,1)S(1)}, bf16[2,256,1024]{2,1,0:T(8,128)(2,1)}, u32[]{:S(2)}) copy-start(bf16[2,256,1024]{2,1,0:T(8,128)(2,1)} %copy-done.2) | copy-start | bytes 3145732
  159.6 3.6 %copy-start.4 = (bf16[4,256,1024]{2,1,0:T(8,128)(2,1)}, bf16[4,256,1024]{2,1,0:T(8,128)(2,1)S(1)}, u32[]{:S(2)}) copy-start(bf16[4,256,1024]{2,1,0:T(8,128)(2,1)S(1)} %collective-permute-done.8.refs_0_) | copy-start | bytes 6291460
  159.6 3.6 %copy-start.5 = (bf16[4,256,1024]{2,1,0:T(8,128)(2,1)}, bf16[4,256,1024]{2,1,0:T(8,128)(2,1)S(1)}, u32[]{:S(2)}) copy-start(bf16[4,256,1024]{2,1,0:T(8,128)(2,1)S(1)} %collective-permute-done.9.refs_1_) | copy-start | bytes 6291460
  159.6 19.8 %collective-permute-start.16 = (bf16[4,256,1024]{2,1,0:T(8,128)(2,1)S(1)}, bf16[4,256,1024]{2,1,0:T(8,128)(2,1)S(1)}, u32[]{:S(2)}, u32[]{:S(2)}) collective-permute-start(bf16[4,256,1024]{2,1,0:T(8,128)(2,1)S(1)} %collective-permute-done.8.refs_0_), channel_id=1, source_target_pairs={{0,1},{1,0},{2,3},{3,2},{4,5},{5,4},{6,7},{7,6}} | collective-permute-start | bytes 6291464 | tf_op jit(solution)/shard_map/ppermute | solution.py:229
  160.2 19.3 %collective-permute-start.17 = (bf16[4,256,1024]{2,1,0:T(8,128)(2,1)S(1)}, bf16[4,256,1024]{2,1,0:T(8,128)(2,1)S(1)}, u32[]{:S(2)}, u32[]{:S(2)}) collective-permute-start(bf16[4,256,1024]{2,1,0:T(8,128)(2,1)S(1)} %collective-permute-done.9.refs_1_), channel_id=1, source_target_pairs={{0,1},{1,0},{2,3},{3,2},{4,5},{5,4},{6,7},{7,6}} | collective-permute-start | bytes 6291464 | tf_op jit(solution)/shard_map/ppermute | solution.py:229
  160.2 34.3 %collective-permute-start = (bf16[2,256,1024]{2,1,0:T(8,128)(2,1)S(1)}, bf16[2,256,1024]{2,1,0:T(8,128)(2,1)S(1)}, u32[]{:S(2)}, u32[]{:S(2)}) collective-permute-start(bf16[2,256,1024]{2,1,0:T(8,128)(2,1)S(1)} %copy-done.1), channel_id=1, source_target_pairs={{0,2},{1,3},{2,0},{3,1},{4,6},{5,7},{6,4},{7,5}} | collective-permute-start | bytes 3145736 | tf_op jit(solution)/shard_map/ppermute | solution.py:229
  161.7 32.8 %collective-permute-start.1 = (bf16[2,256,1024]{2,1,0:T(8,128)(2,1)S(1)}, bf16[2,256,1024]{2,1,0:T(8,128)(2,1)S(1)}, u32[]{:S(2)}, u32[]{:S(2)}) collective-permute-start(bf16[2,256,1024]{2,1,0:T(8,128)(2,1)S(1)} %copy-done.3), channel_id=1, source_target_pairs={{0,4},{1,5},{2,6},{3,7},{4,0},{5,1},{6,2},{7,3}} | collective-permute-start | bytes 3145736 | tf_op jit(solution)/shard_map/ppermute | solution.py:229
  194.5 2.0 copy-start.8
  194.5 2.0 copy-start.10
  194.6 11.2 %collective-permute-start.22 = (bf16[2,256,1024]{2,1,0:T(8,128)(2,1)S(1)}, bf16[2,256,1024]{2,1,0:T(8,128)(2,1)S(1)}, u32[]{:S(2)}, u32[]{:S(2)}) collective-permute-start(bf16[2,256,1024]{2,1,0:T(8,128)(2,1)S(1)} %collective-permute-done.refs_0_), channel_id=1, source_target_pairs={{0,1},{1,0},{2,3},{3,2},{4,5},{5,4},{6,7},{7,6}} | collective-permute-start | bytes 3145736 | tf_op jit(solution)/shard_map/ppermute | solution.py:229
  194.6 11.2 %collective-permute-start.23 = (bf16[2,256,1024]{2,1,0:T(8,128)(2,1)S(1)}, bf16[2,256,1024]{2,1,0:T(8,128)(2,1)S(1)}, u32[]{:S(2)}, u32[]{:S(2)}) collective-permute-start(bf16[2,256,1024]{2,1,0:T(8,128)(2,1)S(1)} %collective-permute-done.1.refs_1_), channel_id=1, source_target_pairs={{0,1},{1,0},{2,3},{3,2},{4,5},{5,4},{6,7},{7,6}} | collective-permute-start | bytes 3145736 | tf_op jit(solution)/shard_map/ppermute | solution.py:229
  195.1 25.1 %collective-permute-start.20 = (bf16[2,256,1024]{2,1,0:T(8,128)(2,1)S(1)}, bf16[2,256,1024]{2,1,0:T(8,128)(2,1)S(1)}, u32[]{:S(2)}, u32[]{:S(2)}) collective-permute-start(bf16[2,256,1024]{2,1,0:T(8,128)(2,1)S(1)} %copy-done.3), channel_id=1, source_target_pairs={{0,2},{1,3},{2,0},{3,1},{4,6},{5,7},{6,4},{7,5}} | collective-permute-start | bytes 3145736 | tf_op jit(solution)/shard_map/ppermute | solution.py:229
  195.6 24.8 %collective-permute-start.21 = (bf16[2,256,1024]{2,1,0:T(8,128)(2,1)S(1)}, bf16[2,256,1024]{2,1,0:T(8,128)(2,1)S(1)}, u32[]{:S(2)}, u32[]{:S(2)}) collective-permute-start(bf16[2,256,1024]{2,1,0:T(8,128)(2,1)S(1)} %copy-done.1), channel_id=1, source_target_pairs={{0,4},{1,5},{2,6},{3,7},{4,0},{5,1},{6,2},{7,3}} | collective-permute-start | bytes 3145736 | tf_op jit(solution)/shard_map/ppermute | solution.py:229
  205.8 15.2 %copy-start.11 = (bf16[2,256,1024]{2,1,0:T(8,128)(2,1)S(1)}, bf16[2,256,1024]{2,1,0:T(8,128)(2,1)}, u32[]{:S(2)}) copy-start(bf16[2,256,1024]{2,1,0:T(8,128)(2,1)} %copy-done.10) | copy-start | bytes 3145732
  205.8 16.7 %copy-start.9 = (bf16[2,256,1024]{2,1,0:T(8,128)(2,1)S(1)}, bf16[2,256,1024]{2,1,0:T(8,128)(2,1)}, u32[]{:S(2)}) copy-start(bf16[2,256,1024]{2,1,0:T(8,128)(2,1)} %copy-done.8) | copy-start | bytes 3145732
  220.2 2.8 %copy-start.12 = (bf16[2,256,1024]{2,1,0:T(8,128)(2,1)}, bf16[2,256,1024]{2,1,0:T(8,128)(2,1)S(1)}, u32[]{:S(2)}) copy-start(bf16[2,256,1024]{2,1,0:T(8,128)(2,1)S(1)} %collective-permute-done.20.refs_0_) | copy-start | bytes 3145732
  220.4 2.6 copy-start.13
  220.4 11.8 %collective-permute-start.24 = (bf16[2,256,1024]{2,1,0:T(8,128)(2,1)S(1)}, bf16[2,256,1024]{2,1,0:T(8,128)(2,1)S(1)}, u32[]{:S(2)}, u32[]{:S(2)}) collective-permute-start(bf16[2,256,1024]{2,1,0:T(8,128)(2,1)S(1)} %collective-permute-done.20.refs_0_), channel_id=1, source_target_pairs={{0,1},{1,0},{2,3},{3,2},{4,5},{5,4},{6,7},{7,6}} | collective-permute-start | bytes 3145736 | tf_op jit(solution)/shard_map/ppermute | solution.py:229
  220.4 11.8 %collective-permute-start.25 = (bf16[2,256,1024]{2,1,0:T(8,128)(2,1)S(1)}, bf16[2,256,1024]{2,1,0:T(8,128)(2,1)S(1)}, u32[]{:S(2)}, u32[]{:S(2)}) collective-permute-start(bf16[2,256,1024]{2,1,0:T(8,128)(2,1)S(1)} %collective-permute-done.21.refs_1_), channel_id=1, source_target_pairs={{0,1},{1,0},{2,3},{3,2},{4,5},{5,4},{6,7},{7,6}} | collective-permute-start | bytes 3145736 | tf_op jit(solution)/shard_map/ppermute | solution.py:229
  221.0 25.1 %collective-permute-start.18 = (bf16[2,256,1024]{2,1,0:T(8,128)(2,1)S(1)}, bf16[2,256,1024]{2,1,0:T(8,128)(2,1)S(1)}, u32[]{:S(2)}, u32[]{:S(2)}) collective-permute-start(bf16[2,256,1024]{2,1,0:T(8,128)(2,1)S(1)} %copy-done.11), channel_id=1, source_target_pairs={{0,2},{1,3},{2,0},{3,1},{4,6},{5,7},{6,4},{7,5}} | collective-permute-start | bytes 3145736 | tf_op jit(solution)/shard_map/ppermute | solution.py:229
  222.4 24.8 %collective-permute-start.19 = (bf16[2,256,1024]{2,1,0:T(8,128)(2,1)S(1)}, bf16[2,256,1024]{2,1,0:T(8,128)(2,1)S(1)}, u32[]{:S(2)}, u32[]{:S(2)}) collective-permute-start(bf16[2,256,1024]{2,1,0:T(8,128)(2,1)S(1)} %copy-done.9), channel_id=1, source_target_pairs={{0,4},{1,5},{2,6},{3,7},{4,0},{5,1},{6,2},{7,3}} | collective-permute-start | bytes 3145736 | tf_op jit(solution)/shard_map/ppermute | solution.py:229
  246.0 1.7 copy-start.14
  247.2 1.0 copy-start.15
  247.2 10.2 %collective-permute-start.26 = (bf16[2,256,1024]{2,1,0:T(8,128)(2,1)S(1)}, bf16[2,256,1024]{2,1,0:T(8,128)(2,1)S(1)}, u32[]{:S(2)}, u32[]{:S(2)}) collective-permute-start(bf16[2,256,1024]{2,1,0:T(8,128)(2,1)S(1)} %collective-permute-done.18.refs_0_), channel_id=1, source_target_pairs={{0,1},{1,0},{2,3},{3,2},{4,5},{5,4},{6,7},{7,6}} | collective-permute-start | bytes 3145736 | tf_op jit(solution)/shard_map/ppermute | solution.py:229
  247.2 10.2 %collective-permute-start.27 = (bf16[2,256,1024]{2,1,0:T(8,128)(2,1)S(1)}, bf16[2,256,1024]{2,1,0:T(8,128)(2,1)S(1)}, u32[]{:S(2)}, u32[]{:S(2)}) collective-permute-start(bf16[2,256,1024]{2,1,0:T(8,128)(2,1)S(1)} %collective-permute-done.19.refs_1_), channel_id=1, source_target_pairs={{0,1},{1,0},{2,3},{3,2},{4,5},{5,4},{6,7},{7,6}} | collective-permute-start | bytes 3145736 | tf_op jit(solution)/shard_map/ppermute | solution.py:229
